TPU v7x, 256 devices: a whole 4x4x8 slice. The times are simulated.
256 devices in a mesh: dp: 32 (over z, x_lo, core), row: 4 (over y), col: 2 (over x_hi).
Axes of the slice: x: 4 (x_hi: 2, x_lo: 2; x = x_hi * 2 + x_lo), y: 4, z: 8, core: 2. Of those that a mesh axis runs over, the one named last changes fastest.
Arguments:
- latents: bfloat16 [32768, 2048], P(('dp', 'col'), 'row'), parts along dimension 0, may hold values from -64 to 64
- norm_gain: float32 [65536], P(('dp', 'row')), parts along dimension 0, may hold values from 0.1 to 1.9
- q_weight: bfloat16 [65536, 2048], P(('dp', 'row'), 'col'), parts along dimension 0, may hold values from -1 to 1
- k_weight: bfloat16 [65536, 2048], P(('dp', 'row'), 'col'), parts along dimension 0, may hold values from -1 to 1
- v_weight: bfloat16 [65536, 2048], P(('dp', 'row'), 'col'), parts along dimension 0, may hold values from -0.125 to 0.125
- out_weight: bfloat16 [65536, 2048], P(('dp', 'col'), 'row'), parts along dimension 0, may hold values from -0.5 to 0.5
Outputs:
- attended: bfloat16 [32768, 2048], P(('dp', 'col'), 'row'), parts along dimension 0
There are 32 independent parts, one for each index of `dp`. A program takes and returns all parts, laid end to end along the dimension named above; each array names one. Nothing has to cross between parts.
All inputs are finite; a program needn't handle non-finite values.
Results may differ from a plain program's by a relative error of at most 0.03.
Values may be sent and summed in bfloat16 or wider, within the bound.
No kernel may reach another device: no remote copies, remote signals or barrier semaphores. Data moves between devices by JAX's collectives and lax.ppermute only.
A program may use at most 64 MiB of HBM per device.

v0:
```python
import jax
import jax.numpy as jnp
from jax import lax
from jax.sharding import PartitionSpec as P

HEAD_DIM = 128
D = 2048


def sent_to_all(shard, axis):
    copies = jnp.broadcast_to(shard, (lax.axis_size(axis), *shard.shape))
    return lax.all_to_all(copies, axis, split_axis=0, concat_axis=0, tiled=True)


def laid_out(parts, dim):
    dims = list(parts.shape[1:])
    dims[dim] *= parts.shape[0]
    return jnp.moveaxis(parts, 0, dim).reshape(dims)


def gathered_copies(shard, axis, dim):
    parts = sent_to_all(shard, axis)
    return laid_out(parts, dim)


def split_up(shard, dim, count):
    before, after = (shard.shape[:dim], shard.shape[dim + 1 :])
    return jnp.moveaxis(shard.reshape(*before, count, -1, *after), dim, 0)


def summed_on_arrival(shard, axis, dim):
    parts = split_up(shard, dim, lax.axis_size(axis))
    arrived = lax.all_to_all(parts, axis, split_axis=0, concat_axis=0, tiled=True)
    return arrived.astype(jnp.float32).sum(axis=0)


def per_device(latents, norm_gain, q_weight, k_weight, v_weight, out_weight):
    wide = latents.astype(jnp.float32)
    squares = jnp.sum(wide * wide, axis=1)
    total = lax.psum(squares, "row")
    normed = (wide * lax.rsqrt(total / D + 1e-06)[:, None] * norm_gain[None, :]).astype(
        jnp.bfloat16
    )
    gathered = gathered_copies(normed, "col", 0)
    row_count = lax.axis_size("row")
    columns = q_weight.shape[1]
    inv_root = 1.0 / jnp.sqrt(jnp.float32(HEAD_DIM))

    def attend(query):
        heads_here = query.shape[1] // HEAD_DIM
        query3 = query.reshape(query.shape[0], heads_here, HEAD_DIM)
        initial = (
            jnp.full((heads_here, query.shape[0]), -1e30, jnp.float32),
            jnp.zeros((heads_here, query.shape[0]), jnp.float32),
            jnp.zeros((heads_here, query.shape[0], HEAD_DIM), jnp.float32),
        )

        def update(carry, pieces, start):
            peak, denom, acc = carry
            keys_part, values_part = pieces
            keys3 = keys_part.reshape(keys_part.shape[0], heads_here, HEAD_DIM)
            values3 = values_part.reshape(values_part.shape[0], heads_here, HEAD_DIM)
            scores = (
                jnp.einsum("qhd,khd->hqk", query3, keys3, preferred_element_type=jnp.float32)
                * inv_root
            )
            fresh = jnp.maximum(peak, jnp.max(scores, axis=2))
            weights = jnp.exp(scores - fresh[:, :, None])
            denom = jnp.sum(weights, axis=2)
            acc = jnp.einsum(
                "hqk,khd->hqd",
                weights.astype(jnp.bfloat16),
                values3,
                preferred_element_type=jnp.float32,
            )
            return (fresh, denom, acc)

        return (initial, update)

    quarter = columns // row_count
    width_rows = q_weight.shape[0]
    joined = jnp.stack(
        [
            q_weight.reshape(width_rows, row_count, quarter),
            k_weight.reshape(width_rows, row_count, quarter),
            v_weight.reshape(width_rows, row_count, quarter),
        ],
        axis=2,
    ).reshape(width_rows, 3 * columns)
    partial_value = jnp.dot(gathered, joined, preferred_element_type=jnp.float32).astype(
        jnp.bfloat16
    )
    reduced = summed_on_arrival(partial_value, "row", 1).astype(jnp.bfloat16)
    query = reduced[:, :quarter]
    initial, update = attend(query)
    peak, denom, acc = update(
        initial, (reduced[:, quarter : 2 * quarter], reduced[:, 2 * quarter :]), 0
    )
    mixed = acc / denom[:, :, None]
    mixed = jnp.transpose(mixed, (1, 0, 2)).reshape(query.shape[0], quarter).astype(jnp.bfloat16)
    terms = jnp.dot(
        gathered_copies(mixed, "row", 1), out_weight, preferred_element_type=jnp.float32
    ).astype(jnp.bfloat16)
    return summed_on_arrival(terms, "col", 0).astype(jnp.bfloat16)


def solution(mesh):
    return jax.shard_map(
        per_device,
        mesh=mesh,
        in_specs=(
            P(("dp", "col"), "row"),
            P(("dp", "row")),
            P(("dp", "row"), "col"),
            P(("dp", "row"), "col"),
            P(("dp", "row"), "col"),
            P(("dp", "col"), "row"),
        ),
        out_specs=P(("dp", "col"), "row"),
        check_vma=False,
    )
```

profile of v0, /device:TPU:130, one launch (start us, length us, event | category | flops | bytes accessed | tf_op | source)
XLA Modules:
  0.0 164.5 jit_solution(10892793753249699081)
XLA Ops:
  0.0 0.0 copy-start
  0.0 1.3 fusion.9
  1.3 10.7 %psum.7 = f32[512]{0:T(512)S(1)} all-reduce(f32[512]{0:T(512)S(1)} %fusion.9), channel_id=1, replica_groups=mesh['dp'=32,'row'=4,'col'=2] {'row'}, use_global_device_ids=true, to_apply=%region_1.0 | all-reduce | flops 512 | bytes 4096 | tf_op jit(solution)/shard_map/psum | solution.py:40
  12.1 1.2 fusion.11
  13.3 1.0 broadcast_in_dim.6
  14.4 4.4 %all-to-all-start = ((bf16[2,512,512]{2,1,0:T(8,128)(2,1)}), bf16[2,512,512]{2,1,0:T(8,128)(2,1)}, u32[]{:S(2)}, u32[]{:S(2)}) async-start(bf16[2,512,512]{2,1,0:T(8,128)(2,1)} %broadcast_in_dim.6), calls=%async_computation | async-start | bytes 2097152 | tf_op jit(solution)/shard_map/all_to_all | solution.py:12
  18.8 1.5 copy.15
  20.3 1.5 copy.16
  21.8 2.3 %copy.17 = bf16[512,1024]{0,1:T(8,128)(2,1)} copy(bf16[512,1024]{1,0:T(8,128)(2,1)} %param.10) | data formatting | bytes 2097152 | tf_op args[4]
  24.1 3.2 %pad_maximum_fusion = bf16[512,4,3,256]{0,3,2,1:T(8,128)(2,1)} fusion(bf16[512,4,1,256]{0,3,2,1:T(8,128)(2,1)} %bitcast.36, bf16[512,4,1,256]{0,3,2,1:T(8,128)(2,1)S(1)} %bitcast.35, bf16[512,4,1,256]{0,3,2,1:T(8,128)(2,1)S(1)} %bitcast.34), kind=kLoop, calls=%fused_computation.9 | loop fusion | flops 3145728 | bytes 6291456 | tf_op jit(solution)/shard_map/stack | solution.py:82
  27.3 4.9 %all-to-all-done = bf16[2,512,512]{2,1,0:T(8,128)(2,1)} async-done(((bf16[2,512,512]{2,1,0:T(8,128)(2,1)}), bf16[2,512,512]{2,1,0:T(8,128)(2,1)}, u32[]{:S(2)}, u32[]{:S(2)}) %all-to-all-start) | async-done | bytes 1048608 | tf_op jit(solution)/shard_map/all_to_all | solution.py:12
  32.2 5.7 %convolution_convert_fusion = bf16[1024,3072]{1,0:T(8,128)(2,1)S(1)} fusion(bf16[1024,512]{1,0:T(8,128)(2,1)} %bitcast, bf16[512,3072]{0,1:T(8,128)(2,1)} %bitcast.37), kind=kOutput, calls=%fused_computation.5 | convolution fusion | flops 3224371200 | bytes 10485760 | tf_op jit(solution)/shard_map/dot_general | solution.py:90
  37.9 0.4 copy.35
  38.3 72.3 %all_to_all.20 = bf16[4,1024,768]{2,1,0:T(8,128)(2,1)} all-to-all(bf16[4,1024,768]{2,1,0:T(8,128)(2,1)S(1)} %bitcast.32), channel_id=1, replica_groups=mesh['dp'=32,'row'=4,'col'=2] {'row'}, dimensions={0} | all-to-all | bytes 12582912 | tf_op jit(solution)/shard_map/all_to_all | solution.py:33
  110.6 4.7 %reduce_sum.43 = bf16[1024,768]{1,0:T(8,128)(2,1)S(1)} reduce(bf16[4,1024,768]{2,1,0:T(8,128)(2,1)} %all_to_all.20, bf16[]{:T(256)} %constant.12.clone.1), dimensions={0}, to_apply=%region_2.0 | reduce | flops 2359296 | bytes 7864322 | tf_op jit(solution)/shard_map/reduce_sum | solution.py:34
  115.3 1.1 fusion.15
  116.4 1.2 copy.21
  117.6 1.2 copy.20
  118.9 0.2 copy.24
  119.1 1.3 multiply_reduce_fusion
  120.4 1.4 fusion
  121.8 1.7 %divide_convert_fusion = bf16[1024,2,128]{0,2,1:T(8,128)(2,1)S(1)} fusion(bf16[1024,2,128]{0,2,1:T(8,128)(2,1)S(1)} %bitcast.43, f32[2,1024,1024]{1,2,0:T(8,128)S(1)} %get-tuple-element.9, f32[2,1024]{1,0:T(2,128)S(1)} %broadcast_maximum_fusion, f32[1024,2]{0,1:T(2,128)S(1)} %bitcast.44), kind=kOutput, calls=%fused_computation.17 | convolution fusion | flops 543686656 | bytes 9453568 | tf_op jit(solution)/shard_map/hqk,khd->hqd/dot_general | solution.py:70
  123.5 0.3 broadcast_in_dim.15
  123.7 25.1 %all_to_all.21 = bf16[4,1024,256]{1,2,0:T(8,128)(2,1)S(1)} all-to-all(bf16[4,1024,256]{1,2,0:T(8,128)(2,1)S(1)} %broadcast_in_dim.15), channel_id=1, replica_groups=mesh['dp'=32,'row'=4,'col'=2] {'row'}, dimensions={0} | all-to-all | bytes 4194304 | tf_op jit(solution)/shard_map/all_to_all | solution.py:12
  148.8 0.0 copy-done
  148.8 1.3 convolution_convert_fusion.1
  150.1 13.3 %all_to_all.22 = bf16[2,512,512]{2,1,0:T(8,128)(2,1)S(1)} all-to-all(bf16[2,512,512]{2,1,0:T(8,128)(2,1)S(1)} %bitcast.41), channel_id=1, replica_groups=mesh['dp'=32,'row'=4,'col'=2] {'col'}, dimensions={0} | all-to-all | bytes 2097152 | tf_op jit(solution)/shard_map/all_to_all | solution.py:33
  163.4 1.1 reduce_sum.45
  (2 shorter events, 0.0 us)
Async XLA Ops:
  0.0 148.8 %copy-start = (bf16[1024,512]{1,0:T(8,128)(2,1)S(1)}, bf16[1024,512]{1,0:T(8,128)(2,1)}, u32[]{:S(2)}) copy-start(bf16[1024,512]{1,0:T(8,128)(2,1)} %param.11) | copy-start | bytes 3145732
  14.4 17.9 %all-to-all-start = ((bf16[2,512,512]{2,1,0:T(8,128)(2,1)}), bf16[2,512,512]{2,1,0:T(8,128)(2,1)}, u32[]{:S(2)}, u32[]{:S(2)}) async-start(bf16[2,512,512]{2,1,0:T(8,128)(2,1)} %broadcast_in_dim.6), calls=%async_computation | async-start | bytes 2097152 | tf_op jit(solution)/shard_map/all_to_all | solution.py:12
where the time goes:
time: 165 us
  blocking collectives  121 us (73%)
  other arithmetic  13 us (8%)
  local copies, waits for them, and re-layouts  10.8 us (7%)
  matrix products  9.94 us (6%)
  waiting for transfers between devices  4.91 us (3%)
  starting transfers between devices  4.4 us (3%)
    all_to_all x2, blocking collectives, summed_on_arrival(): lax.all_to_all(parts, axis, split_axis=0, concat_axis=0, tiled=True)  85.6 us
    all_to_all x1, blocking collectives, sent_to_all(): return lax.all_to_all(copies, axis, split_axis=0, concat_axis=0, tiled=True)  25.1 us
    psum x1, blocking collectives, per_device(): total = lax.psum(squares, 'row')  10.7 us
    reduce_sum x2, other arithmetic, summed_on_arrival(): return arrived.astype(jnp.float32).sum(axis=0)  5.83 us
    dot_general x1, matrix products, per_device(): jnp.dot(gathered, joined, preferred_element_type=jnp.float32)  5.67 us
    unnamed x5, local copies, waits for them, and re-layouts  5.3 us
    all_to_all x1, waiting for transfers between devices, sent_to_all(): return lax.all_to_all(copies, axis, split_axis=0, concat_axis=0, tiled=True)  4.91 us
    all_to_all x1, starting transfers between devices, sent_to_all(): return lax.all_to_all(copies, axis, split_axis=0, concat_axis=0, tiled=True)  4.4 us
  transfers between devices with their start and end apart: 1, of which 1 were waited for; matrix products, arithmetic and copies ran while one was open for 5% of the time, Pallas kernels for 0%

commit v1 on v0

v1 whole, which is shorter than its diff:
```python
import jax
import jax.numpy as jnp
from jax import lax
from jax.experimental import pallas as pl
from jax.experimental.pallas import tpu as pltpu
from jax.sharding import PartitionSpec as P


HEAD_DIM = 128
D = 2048
BF16 = jnp.bfloat16
F32 = jnp.float32

P1 = [(0, 1), (1, 0), (2, 3), (3, 2)]
P2 = [(1, 2), (2, 1), (3, 0), (0, 3)]
OPP = [(0, 2), (1, 3), (2, 0), (3, 1)]
COL = [(0, 1), (1, 0)]
LOG2E = 1.4426950408889634
FIRST_MIB = 61


def ring():
    me = lax.axis_index("row")
    return me, me ^ 1, 3 - me, me ^ 2


ME, FIRST, SECOND, ACROSS = range(4)


def dot(a, b):
    return jnp.dot(a, b, preferred_element_type=F32)


def params(mebibytes):
    return pltpu.CompilerParams(vmem_limit_bytes=mebibytes * 2**20)


VMEM = pl.BlockSpec(memory_space=pltpu.VMEM)
HBM = pl.BlockSpec(memory_space=pltpu.HBM)


PAIR = 2 * HEAD_DIM


def columns_of(ref, start, count):
    return ref[:, pl.ds(pl.multiple_of(start, HEAD_DIM), count)]


def gained(near_ref, gain_ref):
    return (near_ref[...].astype(F32) * gain_ref[...]).astype(BF16)


def local_call(body, shapes, operands, flops, mebibytes=10, in_specs=None, scratch=(), exps=0):
    outs = [jax.ShapeDtypeStruct(shape, dtype) for shape, dtype in shapes]
    results = pl.pallas_call(
        body,
        in_specs=in_specs or [VMEM] * len(operands),
        out_specs=[VMEM] * len(outs),
        out_shape=outs,
        scratch_shapes=list(scratch),
        cost_estimate=pl.CostEstimate(
            flops=flops,
            bytes_accessed=sum(x.size * x.dtype.itemsize for x in list(operands) + outs),
            transcendentals=exps,
        ),
        compiler_params=params(mebibytes),
    )(*operands)
    return results if len(outs) > 1 else results[0]


def first_queries(near, gain, q_weight):
    tokens, width = near.shape

    def body(gain_ref, near_ref, q_ref, out_ref, here, held, sems):
        place = ring()
        copies = [pltpu.make_async_copy(near_ref, here, sems.at[0])]
        for slot, target in enumerate((ACROSS, SECOND)):
            start = pl.multiple_of(PAIR * place[target], PAIR)
            copies.append(
                pltpu.make_async_copy(
                    q_ref.at[:, pl.ds(start, PAIR)],
                    held.at[:, slot * PAIR : (slot + 1) * PAIR],
                    sems.at[slot + 1],
                )
            )
        for copy in copies:
            copy.start()
        copies[0].wait()
        block = gained(here, gain_ref)
        for slot in range(2):
            copies[slot + 1].wait()
            cut = slice(slot * PAIR, (slot + 1) * PAIR)
            out_ref[:, cut] = dot(block, held[:, cut]).astype(BF16)

    return local_call(
        body,
        [((tokens, 2 * PAIR), BF16)],
        (gain, near, q_weight),
        4 * tokens * width * PAIR,
        FIRST_MIB,
        [VMEM, HBM, HBM],
        [
            pltpu.VMEM((tokens, width), BF16),
            pltpu.VMEM((width, 2 * PAIR), BF16),
            pltpu.SemaphoreType.DMA((3,)),
        ],
    )


def folded(gain, k_weight, v_weight):
    width = k_weight.shape[0]

    def body(gain_ref, k_ref, v_ref, pass_ref, stay0_ref, stay1_ref):
        place = ring()
        factor = jnp.broadcast_to(gain_ref[...], (HEAD_DIM, width)).T
        for head in range(2):
            for which, ref in enumerate((k_ref, v_ref)):
                for target, out_ref, start in (
                    (ACROSS, pass_ref, head * PAIR),
                    (FIRST, (stay0_ref, stay1_ref)[head], 0),
                ):
                    block = columns_of(ref, PAIR * place[target] + head * HEAD_DIM, HEAD_DIM)
                    start = start + which * HEAD_DIM
                    out_ref[:, start : start + HEAD_DIM] = (block.astype(F32) * factor).astype(BF16)

    return local_call(
        body,
        [((width, 2 * PAIR), BF16), ((width, PAIR), BF16), ((width, PAIR), BF16)],
        (gain, k_weight, v_weight),
        8 * width * PAIR,
    )


def queries(targets, near, gain, q_weight, addend, out_dtype):
    tokens, width = near.shape
    extra = [] if addend is None else [addend[0]]

    def body(gain_ref, near_ref, q_ref, *refs):
        place = ring()
        here = gained(near_ref, gain_ref)
        for slot, target in enumerate(targets):
            value = dot(here, columns_of(q_ref, PAIR * place[target], PAIR))
            if extra:
                value = value + refs[0][:, addend[1] * PAIR : (addend[1] + 1) * PAIR].astype(F32)
            refs[-1][:, slot * PAIR : (slot + 1) * PAIR] = value.astype(out_dtype)

    return local_call(
        body,
        [((tokens, PAIR * len(targets)), out_dtype)],
        (gain, near, q_weight, *extra),
        2 * tokens * width * PAIR * len(targets),
    )


def keys_values(head, target, place_of_head, pairs, gain, k_weight, v_weight, arrived, out_dtype):
    tokens, width = pairs[0][0].shape

    def body(gain_ref, k_ref, v_ref, arrived_ref, *refs):
        start = PAIR * ring()[target] + head * HEAD_DIM
        weight = jnp.concatenate(
            [columns_of(k_ref, start, HEAD_DIM), columns_of(v_ref, start, HEAD_DIM)], axis=1
        )
        there = arrived_ref[:, place_of_head * PAIR : (place_of_head + 1) * PAIR]
        for index in range(len(pairs)):
            value = dot(gained(refs[2 * index], gain_ref), weight) + dot(refs[2 * index + 1][...], there)
            refs[-1][index * tokens : (index + 1) * tokens, :] = value.astype(out_dtype)

    return local_call(
        body,
        [((tokens * len(pairs), PAIR), out_dtype)],
        (gain, k_weight, v_weight, arrived, *[block for pair in pairs for block in pair]),
        4 * tokens * width * PAIR * len(pairs),
    )


def attend(head, q_own, q_other, kept, far_own, far_other, scale, beside):
    half = far_own.shape[0]
    block = 256
    offset = 0 if beside is None else HEAD_DIM
    operands = [scale, *q_own, *q_other, kept, far_own, far_other]
    operands += [] if beside is None else [beside]

    def body(scale_ref, qa_ref, qb_ref, qc_ref, qd_ref, kept_ref, own_ref, other_ref, *refs):
        out_other_ref, out_own_ref, q_ref, k_ref, v_ref = refs[-5:]
        if beside is not None:
            out_own_ref[:, :HEAD_DIM] = refs[0][...]
        cut = slice(head * HEAD_DIM, (head + 1) * HEAD_DIM)
        for index, (first_ref, second_ref, far_ref) in enumerate(
            ((qa_ref, qb_ref, own_ref), (qc_ref, qd_ref, other_ref))
        ):
            rows = slice(index * half, (index + 1) * half)
            factor = jnp.broadcast_to(scale_ref[:, rows], (HEAD_DIM, half)).T
            query = first_ref[:, cut].astype(F32) + second_ref[:, cut].astype(F32)
            value = kept_ref[rows, :] + far_ref[...].astype(F32)
            q_ref[rows, :] = (query * (factor * (LOG2E / HEAD_DIM**0.5))).astype(BF16)
            k_ref[rows, :] = (value[:, :HEAD_DIM] * factor).astype(BF16)
            v_ref[rows, :] = (value[:, HEAD_DIM:] * factor).astype(BF16)
        for start in list(range(half, 2 * half, block)) + list(range(0, half, block)):
            scores = lax.dot_general(
                q_ref[start : start + block, :],
                k_ref[...],
                (((1,), (1,)), ((), ())),
                preferred_element_type=F32,
            )
            weights = jnp.exp2(scores - jnp.max(scores, axis=1, keepdims=True))
            denom = jnp.sum(weights, axis=1, keepdims=True)
            mixed = (dot(weights.astype(BF16), v_ref[...]) / denom).astype(BF16)
            if start >= half:
                out_other_ref[start - half : start - half + block, :] = mixed
            else:
                out_own_ref[start : start + block, offset:] = mixed

    return local_call(
        body,
        [((half, HEAD_DIM), BF16), ((half, HEAD_DIM + offset), BF16)],
        operands,
        16 * half * half * HEAD_DIM,
        14,
        scratch=[pltpu.VMEM((2 * half, HEAD_DIM), BF16)] * 3,
        exps=4 * half * half,
    )


def output_product(terms, weights, extra, out_dtype):
    tokens = terms[0][0].shape[0]
    columns = sum(x.shape[1] for x in weights[0])
    bounds = [0]
    for pieces in weights:
        bounds.append(bounds[-1] + len(pieces))
    operands = [x for pieces in weights for x in pieces] + [term[0] for term in terms]
    operands += [] if extra is None else [extra]

    def body(*refs):
        spot = ring()
        piece_refs = refs[bounds[-1] : bounds[-1] + len(terms)]

        def operand(index):
            _, place, which, head, source = terms[index]
            rows = pl.ds(pl.multiple_of((2 * spot[source] + head) * HEAD_DIM, HEAD_DIM), HEAD_DIM)
            parts = [ref[rows, :] for ref in refs[bounds[which] : bounds[which + 1]]]
            return (
                piece_refs[index][:, place * HEAD_DIM : (place + 1) * HEAD_DIM],
                parts[0] if len(parts) == 1 else jnp.concatenate(parts, axis=1),
            )

        total = None if extra is None else refs[-2][...]
        for index in range(0, len(terms), 2):
            (left, top), (right, bottom) = operand(index), operand(index + 1)
            term = dot(
                jnp.concatenate([left, right], axis=1), jnp.concatenate([top, bottom], axis=0)
            )
            total = term if total is None else total + term
        refs[-1][...] = total.astype(out_dtype)

    return local_call(
        body, [((tokens, columns), out_dtype)], operands, 2 * tokens * columns * HEAD_DIM * len(terms), 12
    )


def sublayer(latents, norm_gain, q_weight, k_weight, v_weight, out_weight):
    gain = norm_gain[None, :]
    own = latents
    own1 = lax.ppermute(own, "row", P1)
    other = lax.ppermute(own, "col", COL)

    q_own = lax.ppermute(first_queries(own, gain, q_weight), "row", P2)
    both = (ACROSS, SECOND)
    q_other = lax.ppermute(queries(both, other, gain, q_weight, None, BF16), "row", P2)
    end_own = lax.ppermute(queries((FIRST,), own, gain, q_weight, (q_own, 0), BF16), "row", P1)
    end_other = lax.ppermute(queries((FIRST,), other, gain, q_weight, (q_other, 0), BF16), "row", P1)
    kept_q_own = queries((ME,), own, gain, q_weight, (q_own, 1), F32)
    kept_q_other = queries((ME,), other, gain, q_weight, (q_other, 1), F32)

    pass_block, stay_block0, stay_block1 = folded(gain, k_weight, v_weight)
    passed = lax.ppermute(pass_block, "row", P1)
    stay0 = lax.ppermute(stay_block0, "row", P1)
    stay1 = lax.ppermute(stay_block1, "row", P1)
    other1 = lax.ppermute(own1, "col", COL)

    def partial(head, target, place, pairs, arrived, out_dtype):
        return keys_values(head, target, place, pairs, gain, k_weight, v_weight, arrived, out_dtype)

    def sent_partial(head, pair):
        value = partial(head, SECOND, head, [pair], passed, BF16)
        return lax.ppermute(value, "row", P2)

    far0_own = sent_partial(0, (own, own1))
    far0_other = sent_partial(0, (other, other1))
    far1_own = sent_partial(1, (own, own1))
    far1_other = sent_partial(1, (other, other1))
    all_pairs = [(own, own1), (other, other1)]
    kept0 = partial(0, ME, 0, all_pairs, stay0, F32)
    kept1 = partial(1, ME, 0, all_pairs, stay1, F32)

    square = lambda x: jnp.sum(jnp.square(x.astype(F32)), axis=1)
    total = jnp.concatenate([square(own) + square(own1), square(other) + square(other1)])
    total = total + lax.ppermute(total, "row", P2)
    scale = lax.rsqrt(total / D + 1e-06)[None, :]

    def from_all(value):
        return [value, lax.ppermute(value, "row", P1), lax.ppermute(value, "row", P2), lax.ppermute(value, "row", OPP)]

    q_parts = ((kept_q_own, end_own), (kept_q_other, end_other))
    other0, own0 = attend(0, *q_parts, kept0, far0_own, far0_other, scale, None)
    partner0 = lax.ppermute(other0, "col", COL)
    own0_all = from_all(own0)
    other1_mixed, middle = attend(1, *q_parts, kept1, far1_own, far1_other, scale, partner0)
    partner1 = lax.ppermute(other1_mixed, "col", COL)
    middle_all = from_all(middle)
    partner1_all = from_all(partner1)

    half = out_weight.shape[1] // 2
    here = [out_weight]
    there = [lax.ppermute(out_weight[:, :half], "col", COL), lax.ppermute(out_weight[:, half:], "col", COL)]
    terms = [(x, 0, 0, 0, source) for source, x in enumerate(own0_all)]
    total = output_product(terms, [here], None, F32)
    terms = [(x, 0, 1, 0, source) for source, x in enumerate(middle_all)]
    terms += [(x, 1, 0, 1, source) for source, x in enumerate(middle_all)]
    total = output_product(terms, [here, there], total, F32)
    terms = [(x, 0, 0, 1, source) for source, x in enumerate(partner1_all)]
    return output_product(terms, [there], total, BF16)


def solution(mesh):
    return jax.shard_map(
        sublayer,
        mesh=mesh,
        in_specs=(
            P(("dp", "col"), "row"),
            P(("dp", "row")),
            P(("dp", "row"), "col"),
            P(("dp", "row"), "col"),
            P(("dp", "row"), "col"),
            P(("dp", "col"), "row"),
        ),
        out_specs=P(("dp", "col"), "row"),
        check_vma=False,
    )
```

time: 165 us -> 96.2 us (0.58)
  blocking collectives: 121 us -> 0 us
  starting transfers between devices: 4.4 us -> 46.6 us
  waiting for transfers between devices: 4.91 us -> 26.1 us
  Pallas kernels: 0 us -> 20.1 us
  other arithmetic: 13 us -> 1.78 us
  local copies, waits for them, and re-layouts: 10.8 us -> 0.1 us
  matrix products: 9.94 us -> 0 us
    all_to_all x3 -> x0, blocking collectives: 111 us -> none  [the longest x2 85.6 us: summed_on_arrival(): lax.all_to_all(parts, axis, split_axis=0, concat_axis=0, tiled=True)]
    ppermute x0 -> x28, starting transfers between devices: none -> 46.6 us  [the longest x4 7.46 us: sent_partial(): return lax.ppermute(value, 'row', P2)]
    ppermute x0 -> x28, waiting for transfers between devices: none -> 26.1 us  [the longest x1 4.79 us: sublayer(): partner0 = lax.ppermute(other0, 'col', COL)]
    pallas_call x0 -> x18, Pallas kernels: none -> 20.1 us  [local_call(): pl.pallas_call(body, in_specs=in_specs or [VMEM] * len(operands), out_spe...]
    psum x1 -> x0, blocking collectives: 10.7 us -> none  [per_device(): total = lax.psum(squares, 'row')]
    dot_general x4 -> x0, matrix products: 9.94 us -> none  [the longest x1 5.67 us: per_device(): jnp.dot(gathered, joined, preferred_element_type=jnp.float32)]
    reduce_sum x4, other arithmetic: 8.52 us -> 1.75 us  [sublayer(): square = lambda x: jnp.sum(jnp.square(x.astype(F32)), axis=1)]
    unnamed x5 -> x12, local copies, waits for them, and re-layouts: 5.3 us -> 0.03 us
  transfers between devices with their start and end apart: 1 -> 28, of which waited for: 1 -> 8; matrix products, arithmetic and copies ran while one was open for 5% -> 2% of each run, Pallas kernels for 0% -> 20%
where the time goes in v1:
time: 96.2 us; the launch traced here: 94.9 us
  starting transfers between devices  46.6 us (48%)
  waiting for transfers between devices  26.1 us (27%)
  Pallas kernels  20.1 us (21%)
  other arithmetic  1.78 us (2%)
    pallas_call x18, Pallas kernels, local_call(): pl.pallas_call(body, in_specs=in_specs or [VMEM] * len(operands), out_spe...  20.1 us
    ppermute x4, starting transfers between devices, sent_partial(): return lax.ppermute(value, 'row', P2)  7.46 us
    ppermute x3, starting transfers between devices, from_all(): lax.ppermute(value, 'row', P2)  7.17 us
    ppermute x3, starting transfers between devices, from_all(): lax.ppermute(value, 'row', OPP)  4.92 us
    ppermute x1, waiting for transfers between devices, sublayer(): partner0 = lax.ppermute(other0, 'col', COL)  4.79 us
    ppermute x1, waiting for transfers between devices, sublayer(): passed = lax.ppermute(pass_block, 'row', P1)  4.21 us
    ppermute x4, waiting for transfers between devices, sent_partial(): return lax.ppermute(value, 'row', P2)  3.71 us
    ppermute x3, starting transfers between devices, from_all(): lax.ppermute(value, 'row', P1)  3.65 us
  transfers between devices with their start and end apart: 28, of which 8 were waited for; matrix products, arithmetic and copies ran while one was open for 2% of the time, Pallas kernels for 20%

profile of v1, /device:TPU:130, one launch (start us, length us, event | category | flops | bytes accessed | tf_op | source)
XLA Modules:
  0.0 94.9 jit_solution(9983255626411404123)
XLA Ops:
  0.0 2.1 %collective-permute-start.3 = (bf16[512,512]{1,0:T(8,128)(2,1)}, bf16[512,512]{1,0:T(8,128)(2,1)S(1)}, u32[]{:S(2)}, u32[]{:S(2)}) collective-permute-start(bf16[512,512]{1,0:T(8,128)(2,1)} %refs_0_.9), channel_id=1, source_target_pairs={{0,1},{1,0},{2,3},{3,2},{4,5},{5,4},{6,7},{7,6},{8,9},{9,8},{10,11... | collective-permute-start | bytes 1572872 | tf_op jit(solution)/shard_map/ppermute | solution.py:264
  2.1 1.6 %collective-permute-start.2 = (bf16[512,512]{1,0:T(8,128)(2,1)}, bf16[512,512]{1,0:T(8,128)(2,1)}, u32[]{:S(2)}, u32[]{:S(2)}) collective-permute-start(bf16[512,512]{1,0:T(8,128)(2,1)} %refs_0_.9), channel_id=1, source_target_pairs={{0,2},{2,0},{4,6},{6,4},{1,3},{3,1},{5,7},{7,5},{8,10},{10,8},{12,... | collective-permute-start | bytes 1572872 | tf_op jit(solution)/shard_map/ppermute | solution.py:263
  3.7 3.7 %shard_map.64 = bf16[512,512]{1,0:T(8,128)(2,1)} custom-call(f32[1,512]{1,0:T(1,128)} %bitcast.2, bf16[512,512]{1,0:T(8,128)(2,1)} %refs_0_.9, bf16[512,1024]{1,0:T(8,128)(2,1)} %q_ref.11), custom_call_target="tpu_custom_call" | custom-call | flops 268435456 | bytes 2099200 | tf_op jit(solution)/shard_map/pallas_call | solution.py:55
  7.4 0.0 copy-start.2
  7.4 2.3 %collective-permute-start.6 = (bf16[512,512]{1,0:T(8,128)(2,1)}, bf16[512,512]{1,0:T(8,128)(2,1)S(1)}, u32[]{:S(2)}, u32[]{:S(2)}) collective-permute-start(bf16[512,512]{1,0:T(8,128)(2,1)} %shard_map.64), channel_id=1, source_target_pairs={{2,4},{4,2},{6,0},{0,6},{3,5},{5,3},{7,1},{1,7},{10,12},{12,10},{1... | collective-permute-start | bytes 1572872 | tf_op jit(solution)/shard_map/ppermute | solution.py:266
  9.7 0.4 shard_map.70
  10.1 0.8 collective-permute-start.11
  10.9 1.3 %collective-permute-start.14 = (bf16[512,256]{1,0:T(8,128)(2,1)S(1)}, bf16[512,256]{1,0:T(8,128)(2,1)S(1)}, u32[]{:S(2)}, u32[]{:S(2)}) collective-permute-start(bf16[512,256]{1,0:T(8,128)(2,1)S(1)} %get-tuple-element.14), channel_id=1, source_target_pairs={{0,2},{2,0},{4,6},{6,4},{1,3},{3,1},{5,7},{7,5},{8,10},{10,8},{12,... | collective-permute-start | bytes 786440 | tf_op jit(solution)/shard_map/ppermute | solution.py:276
  12.2 3.2 %collective-permute-done.3.near_ref.refs_2_.refs_0_ = bf16[512,512]{1,0:T(8,128)(2,1)S(1)} collective-permute-done((bf16[512,512]{1,0:T(8,128)(2,1)}, bf16[512,512]{1,0:T(8,128)(2,1)S(1)}, u32[]{:S(2)}, u32[]{:S(2)}) %collective-permute-start.3) | collective-permute-done | bytes 524320 | tf_op jit(solution)/shard_map/ppermute | solution.py:264
  15.4 0.5 shard_map.67
  15.8 0.0 copy-start.3
  15.9 3.1 %collective-permute-start.8 = (bf16[512,512]{1,0:T(8,128)(2,1)S(1)}, bf16[512,512]{1,0:T(8,128)(2,1)S(1)}, u32[]{:S(2)}, u32[]{:S(2)}) collective-permute-start(bf16[512,512]{1,0:T(8,128)(2,1)S(1)} %shard_map.67), channel_id=1, source_target_pairs={{2,4},{4,2},{6,0},{0,6},{3,5},{5,3},{7,1},{1,7},{10,12},{12,10},{1... | collective-permute-start | bytes 1572872 | tf_op jit(solution)/shard_map/ppermute | solution.py:268
  19.0 0.0 collective-permute-done.2.refs_1_
  19.0 2.1 %collective-permute-start.4 = (bf16[512,512]{1,0:T(8,128)(2,1)}, bf16[512,512]{1,0:T(8,128)(2,1)S(1)}, u32[]{:S(2)}, u32[]{:S(2)}) collective-permute-start(bf16[512,512]{1,0:T(8,128)(2,1)} %collective-permute-done.2.refs_1_), channel_id=1, source_target_pairs={{0,1},{1,0},{2,3},{3,2},{4,5},{5,4},{6,7},{7,6},{8,9},{9,8},{10,11... | collective-permute-start | bytes 1572872 | tf_op jit(solution)/shard_map/ppermute | solution.py:278
  21.1 0.1 fusion
  21.2 0.2 multiply_reduce_fusion.3
  21.3 2.4 %collective-permute-done.6.refs_0_ = bf16[512,512]{1,0:T(8,128)(2,1)S(1)} collective-permute-done((bf16[512,512]{1,0:T(8,128)(2,1)}, bf16[512,512]{1,0:T(8,128)(2,1)S(1)}, u32[]{:S(2)}, u32[]{:S(2)}) %collective-permute-start.6) | collective-permute-done | bytes 524320 | tf_op jit(solution)/shard_map/ppermute | solution.py:266
  23.7 0.3 shard_map.66
  24.1 0.1 collective-permute-start.7
  24.2 4.2 %collective-permute-done.11.arrived_ref = bf16[512,512]{1,0:T(8,128)(2,1)S(1)} collective-permute-done((bf16[512,512]{1,0:T(8,128)(2,1)S(1)}, bf16[512,512]{1,0:T(8,128)(2,1)S(1)}, u32[]{:S(2)}, u32[]{:S(2)}) %collective-permute-start.11) | collective-permute-done | bytes 524320 | tf_op jit(solution)/shard_map/ppermute | solution.py:275
  28.4 1.5 %shard_map.75 = bf16[512,256]{1,0:T(8,128)(2,1)S(1)} custom-call(f32[1,512]{1,0:T(1,128)S(1)} %bitcast.6, bf16[512,1024]{1,0:T(8,128)(2,1)S(1)} %copy-done, bf16[512,1024]{1,0:T(8,128)(2,1)S(1)} %copy-done.1, bf16[512,512]{1,0:T(8,128)(2,1)S(1)} %collective-permute-done.11.arrived_ref, bf16[512,512]{1,0:T(8,128)(2,1)S(1)} %copy-done.3, ...), custom_call_target="tpu_custom_call" | custom-call | flops 268435456 | bytes 3934208 | tf_op jit(solution)/shard_map/pallas_call | solution.py:55
  29.9 3.1 %collective-permute-start.15 = (bf16[512,256]{1,0:T(8,128)(2,1)S(1)}, bf16[512,256]{1,0:T(8,128)(2,1)S(1)}, u32[]{:S(2)}, u32[]{:S(2)}) collective-permute-start(bf16[512,256]{1,0:T(8,128)(2,1)S(1)} %shard_map.75), channel_id=1, source_target_pairs={{2,4},{4,2},{6,0},{0,6},{3,5},{5,3},{7,1},{1,7},{10,12},{12,10},{1... | collective-permute-start | bytes 786440 | tf_op jit(solution)/shard_map/ppermute | solution.py:285
  33.0 1.2 %multiply_reduce_fusion.2 = f32[512]{0:T(512)S(1)} fusion(bf16[512,512]{1,0:T(8,128)(2,1)} %collective-permute-done.2.refs_1_), kind=kLoop, calls=%fused_computation.2 | loop fusion | flops 785920 | bytes 526336 | tf_op jit(solution)/shard_map/reduce_sum | solution.py:295
  34.2 0.3 shard_map.65.qa_ref
  34.5 1.5 %shard_map.72 = bf16[512,256]{1,0:T(8,128)(2,1)S(1)} custom-call(f32[1,512]{1,0:T(1,128)S(1)} %bitcast.8, bf16[512,1024]{1,0:T(8,128)(2,1)S(1)} %copy-done, bf16[512,1024]{1,0:T(8,128)(2,1)S(1)} %copy-done.1, bf16[512,512]{1,0:T(8,128)(2,1)S(1)} %collective-permute-done.11.arrived_ref, bf16[512,512]{1,0:T(8,128)(2,1)S(1)} %copy-done.3, ...), custom_call_target="tpu_custom_call" | custom-call | flops 268435456 | bytes 3934208 | tf_op jit(solution)/shard_map/pallas_call | solution.py:55
  36.0 0.2 multiply_reduce_fusion.1
  36.2 0.3 shard_map.69
  36.5 0.2 collective-permute-start.9
  36.8 0.4 shard_map.76
  37.2 1.1 %collective-permute-start.16 = (bf16[512,256]{1,0:T(8,128)(2,1)S(1)}, bf16[512,256]{1,0:T(8,128)(2,1)S(1)}, u32[]{:S(2)}, u32[]{:S(2)}) collective-permute-start(bf16[512,256]{1,0:T(8,128)(2,1)S(1)} %shard_map.76), channel_id=1, source_target_pairs={{2,4},{4,2},{6,0},{0,6},{3,5},{5,3},{7,1},{1,7},{10,12},{12,10},{1... | collective-permute-start | bytes 786440 | tf_op jit(solution)/shard_map/ppermute | solution.py:285
  38.3 0.2 multiply_reduce_fusion
  38.5 0.4 shard_map.73
  39.0 2.5 %collective-permute-start.5 = (f32[1024]{0:T(1024)S(1)}, f32[1024]{0:T(1024)S(1)}, u32[]{:S(2)}, u32[]{:S(2)}) collective-permute-start(f32[1024]{0:T(1024)S(1)} %pad_maximum_fusion), channel_id=1, source_target_pairs={{2,4},{4,2},{6,0},{0,6},{3,5},{5,3},{7,1},{1,7},{10,12},{12,10},{1... | collective-permute-start | bytes 12296 | tf_op jit(solution)/shard_map/ppermute | solution.py:297
  41.5 1.7 %shard_map.74.kept_ref = f32[1024,256]{1,0:T(8,128)S(1)} custom-call(f32[1,512]{1,0:T(1,128)S(1)} %bitcast.12, bf16[512,1024]{1,0:T(8,128)(2,1)S(1)} %copy-done, bf16[512,1024]{1,0:T(8,128)(2,1)S(1)} %copy-done.1, bf16[512,256]{1,0:T(8,128)(2,1)S(1)} %collective-permute-done.14.arrived_ref, bf16[512,512]{1,0:T(8,128)(2,1)S(1)} %copy-done.3, ...), custom_call_target="tpu_custom_call" | custom-call | flops 536870912 | bytes 5507072 | tf_op jit(solution)/shard_map/pallas_call | solution.py:55
  43.2 0.3 shard_map.68.qc_ref
  43.5 0.8 collective-permute-start.10
  44.3 0.0 collective-permute-done.15.own_ref
  44.3 1.4 %collective-permute-start.1 = (bf16[1024,256]{1,0:T(8,128)(2,1)S(1)}, bf16[1024,256]{1,0:T(8,128)(2,1)S(1)}, u32[]{:S(2)}, u32[]{:S(2)}) collective-permute-start(bf16[1024,256]{1,0:T(8,128)(2,1)S(1)} %get-tuple-element.19), channel_id=1, source_target_pairs={{0,1},{1,0},{2,3},{3,2},{4,5},{5,4},{6,7},{7,6},{8,9},{9,8},{10,11... | collective-permute-start | bytes 1572872 | tf_op jit(solution)/shard_map/ppermute | solution.py:314
  45.7 2.1 %collective-permute-start = (bf16[1024,256]{1,0:T(8,128)(2,1)S(1)}, bf16[1024,256]{1,0:T(8,128)(2,1)S(1)}, u32[]{:S(2)}, u32[]{:S(2)}) collective-permute-start(bf16[1024,256]{1,0:T(8,128)(2,1)S(1)} %get-tuple-element.20), channel_id=1, source_target_pairs={{0,1},{1,0},{2,3},{3,2},{4,5},{5,4},{6,7},{7,6},{8,9},{9,8},{10,11... | collective-permute-start | bytes 1572872 | tf_op jit(solution)/shard_map/ppermute | solution.py:314
  47.9 0.0 collective-permute-done.9.qd_ref
  47.9 0.6 collective-permute-start.12
  48.5 0.0 collective-permute-done.16.other_ref
  48.5 2.6 %collective-permute-start.13 = (bf16[512,256]{1,0:T(8,128)(2,1)S(1)}, bf16[512,256]{1,0:T(8,128)(2,1)S(1)}, u32[]{:S(2)}, u32[]{:S(2)}) collective-permute-start(bf16[512,256]{1,0:T(8,128)(2,1)S(1)} %shard_map.73), channel_id=1, source_target_pairs={{2,4},{4,2},{6,0},{0,6},{3,5},{5,3},{7,1},{1,7},{10,12},{12,10},{1... | collective-permute-start | bytes 786440 | tf_op jit(solution)/shard_map/ppermute | solution.py:285
  51.1 2.2 %shard_map.77 = (bf16[512,128]{1,0:T(8,128)(2,1)S(1)}, bf16[512,128]{1,0:T(8,128)(2,1)S(1)}) custom-call(f32[1,1024]{1,0:T(1,128)S(1)} %bitcast.15, f32[512,256]{1,0:T(8,128)S(1)} %shard_map.65.qa_ref, bf16[512,256]{1,0:T(8,128)(2,1)S(1)} %collective-permute-done.7.qb_ref, f32[512,256]{1,0:T(8,128)S(1)} %shard_map.68.qc_ref, ...), custom_call_target="tpu_custom_call" | custom-call | flops 536870912 | bytes 3411968 | tf_op jit(solution)/shard_map/pallas_call | solution.py:55
  53.4 1.5 %collective-permute-start.17 = (bf16[512,128]{1,0:T(8,128)(2,1)S(1)}, bf16[512,128]{1,0:T(8,128)(2,1)S(1)}, u32[]{:S(2)}, u32[]{:S(2)}) collective-permute-start(bf16[512,128]{1,0:T(8,128)(2,1)S(1)} %get-tuple-element.15), channel_id=1, source_target_pairs={{0,1},{1,0},{2,3},{3,2},{4,5},{5,4},{6,7},{7,6},{8,9},{9,8},{10,11... | collective-permute-start | bytes 393224 | tf_op jit(solution)/shard_map/ppermute | solution.py:305
  54.9 1.7 %shard_map.71.kept_ref = f32[1024,256]{1,0:T(8,128)S(1)} custom-call(f32[1,512]{1,0:T(1,128)S(1)} %bitcast.14, bf16[512,1024]{1,0:T(8,128)(2,1)S(1)} %copy-done, bf16[512,1024]{1,0:T(8,128)(2,1)S(1)} %copy-done.1, bf16[512,256]{1,0:T(8,128)(2,1)S(1)} %collective-permute-done.10.arrived_ref, bf16[512,512]{1,0:T(8,128)(2,1)S(1)} %copy-done.3, ...), custom_call_target="tpu_custom_call" | custom-call | flops 536870912 | bytes 5507072 | tf_op jit(solution)/shard_map/pallas_call | solution.py:55
  56.6 0.7 collective-permute-start.27
  57.4 3.7 %collective-permute-done.13.other_ref = bf16[512,256]{1,0:T(8,128)(2,1)S(1)} collective-permute-done((bf16[512,256]{1,0:T(8,128)(2,1)S(1)}, bf16[512,256]{1,0:T(8,128)(2,1)S(1)}, u32[]{:S(2)}, u32[]{:S(2)}) %collective-permute-start.13) | collective-permute-done | bytes 262176 | tf_op jit(solution)/shard_map/ppermute | solution.py:285
  61.1 3.7 %collective-permute-start.26 = (bf16[512,128]{1,0:T(8,128)(2,1)S(1)}, bf16[512,128]{1,0:T(8,128)(2,1)S(1)}, u32[]{:S(2)}, u32[]{:S(2)}) collective-permute-start(bf16[512,128]{1,0:T(8,128)(2,1)S(1)} %get-tuple-element.18.refs_1_), channel_id=1, source_target_pairs={{2,4},{4,2},{6,0},{0,6},{3,5},{5,3},{7,1},{1,7},{10,12},{12,10},{1... | collective-permute-start | bytes 393224 | tf_op jit(solution)/shard_map/ppermute | solution.py:301
  64.8 4.8 %collective-permute-done.17.refs_0_ = bf16[512,128]{1,0:T(8,128)(2,1)S(1)} collective-permute-done((bf16[512,128]{1,0:T(8,128)(2,1)S(1)}, bf16[512,128]{1,0:T(8,128)(2,1)S(1)}, u32[]{:S(2)}, u32[]{:S(2)}) %collective-permute-start.17) | collective-permute-done | bytes 131104 | tf_op jit(solution)/shard_map/ppermute | solution.py:305
  69.6 2.3 %shard_map.78 = (bf16[512,128]{1,0:T(8,128)(2,1)S(1)}, bf16[512,256]{1,0:T(8,128)(2,1)S(1)}) custom-call(f32[1,1024]{1,0:T(1,128)S(1)} %bitcast.16, f32[512,256]{1,0:T(8,128)S(1)} %shard_map.65.qa_ref, bf16[512,256]{1,0:T(8,128)(2,1)S(1)} %collective-permute-done.7.qb_ref, f32[512,256]{1,0:T(8,128)S(1)} %shard_map.68.qc_ref, ...), custom_call_target="tpu_custom_call" | custom-call | flops 536870912 | bytes 3674112 | tf_op jit(solution)/shard_map/pallas_call | solution.py:55
  71.9 1.9 %collective-permute-start.24 = (bf16[512,256]{1,0:T(8,128)(2,1)S(1)}, bf16[512,256]{1,0:T(8,128)(2,1)S(1)}, u32[]{:S(2)}, u32[]{:S(2)}) collective-permute-start(bf16[512,256]{1,0:T(8,128)(2,1)S(1)} %get-tuple-element.17.refs_3_.refs_7_), channel_id=1, source_target_pairs={{0,4},{2,6},{4,0},{6,2},{1,5},{3,7},{5,1},{7,3},{8,12},{10,14},{12... | collective-permute-start | bytes 786440 | tf_op jit(solution)/shard_map/ppermute | solution.py:301
  73.8 2.3 %collective-permute-start.23 = (bf16[512,256]{1,0:T(8,128)(2,1)S(1)}, bf16[512,256]{1,0:T(8,128)(2,1)S(1)}, u32[]{:S(2)}, u32[]{:S(2)}) collective-permute-start(bf16[512,256]{1,0:T(8,128)(2,1)S(1)} %get-tuple-element.17.refs_3_.refs_7_), channel_id=1, source_target_pairs={{2,4},{4,2},{6,0},{0,6},{3,5},{5,3},{7,1},{1,7},{10,12},{12,10},{1... | collective-permute-start | bytes 786440 | tf_op jit(solution)/shard_map/ppermute | solution.py:301
  76.2 1.5 %collective-permute-start.18 = (bf16[512,128]{1,0:T(8,128)(2,1)S(1)}, bf16[512,128]{1,0:T(8,128)(2,1)S(1)}, u32[]{:S(2)}, u32[]{:S(2)}) collective-permute-start(bf16[512,128]{1,0:T(8,128)(2,1)S(1)} %get-tuple-element.16), channel_id=1, source_target_pairs={{0,1},{1,0},{2,3},{3,2},{4,5},{5,4},{6,7},{7,6},{8,9},{9,8},{10,11... | collective-permute-start | bytes 393224 | tf_op jit(solution)/shard_map/ppermute | solution.py:308
  77.7 1.9 %collective-permute-start.25 = (bf16[512,128]{1,0:T(8,128)(2,1)S(1)}, bf16[512,128]{1,0:T(8,128)(2,1)S(1)}, u32[]{:S(2)}, u32[]{:S(2)}) collective-permute-start(bf16[512,128]{1,0:T(8,128)(2,1)S(1)} %get-tuple-element.18.refs_1_), channel_id=1, source_target_pairs={{0,2},{2,0},{4,6},{6,4},{1,3},{3,1},{5,7},{7,5},{8,10},{10,8},{12,... | collective-permute-start | bytes 393224 | tf_op jit(solution)/shard_map/ppermute | solution.py:301
  79.6 3.1 %collective-permute-done.18.refs_2_ = bf16[512,128]{1,0:T(8,128)(2,1)S(1)} collective-permute-done((bf16[512,128]{1,0:T(8,128)(2,1)S(1)}, bf16[512,128]{1,0:T(8,128)(2,1)S(1)}, u32[]{:S(2)}, u32[]{:S(2)}) %collective-permute-start.18) | collective-permute-done | bytes 131104 | tf_op jit(solution)/shard_map/ppermute | solution.py:308
  82.7 2.3 %collective-permute-start.21 = (bf16[512,128]{1,0:T(8,128)(2,1)S(1)}, bf16[512,128]{1,0:T(8,128)(2,1)S(1)}, u32[]{:S(2)}, u32[]{:S(2)}) collective-permute-start(bf16[512,128]{1,0:T(8,128)(2,1)S(1)} %collective-permute-done.18.refs_2_), channel_id=1, source_target_pairs={{0,4},{2,6},{4,0},{6,2},{1,5},{3,7},{5,1},{7,3},{8,12},{10,14},{12... | collective-permute-start | bytes 393224 | tf_op jit(solution)/shard_map/ppermute | solution.py:301
  85.0 2.5 %collective-permute-done.25.refs_2_ = bf16[512,128]{1,0:T(8,128)(2,1)S(1)} collective-permute-done((bf16[512,128]{1,0:T(8,128)(2,1)S(1)}, bf16[512,128]{1,0:T(8,128)(2,1)S(1)}, u32[]{:S(2)}, u32[]{:S(2)}) %collective-permute-start.25) | collective-permute-done | bytes 131104 | tf_op jit(solution)/shard_map/ppermute | solution.py:301
  87.5 1.1 %collective-permute-start.20 = (bf16[512,128]{1,0:T(8,128)(2,1)S(1)}, bf16[512,128]{1,0:T(8,128)(2,1)S(1)}, u32[]{:S(2)}, u32[]{:S(2)}) collective-permute-start(bf16[512,128]{1,0:T(8,128)(2,1)S(1)} %collective-permute-done.18.refs_2_), channel_id=1, source_target_pairs={{2,4},{4,2},{6,0},{0,6},{3,5},{5,3},{7,1},{1,7},{10,12},{12,10},{1... | collective-permute-start | bytes 393224 | tf_op jit(solution)/shard_map/ppermute | solution.py:301
  88.6 1.7 %collective-permute-start.19 = (bf16[512,128]{1,0:T(8,128)(2,1)S(1)}, bf16[512,128]{1,0:T(8,128)(2,1)S(1)}, u32[]{:S(2)}, u32[]{:S(2)}) collective-permute-start(bf16[512,128]{1,0:T(8,128)(2,1)S(1)} %collective-permute-done.18.refs_2_), channel_id=1, source_target_pairs={{0,2},{2,0},{4,6},{6,4},{1,3},{3,1},{5,7},{7,5},{8,10},{10,8},{12,... | collective-permute-start | bytes 393224 | tf_op jit(solution)/shard_map/ppermute | solution.py:301
  90.3 0.4 shard_map.79.refs_11_
  90.8 0.7 shard_map.80.refs_6_
  91.5 2.2 %collective-permute-done.20.refs_4_ = bf16[512,128]{1,0:T(8,128)(2,1)S(1)} collective-permute-done((bf16[512,128]{1,0:T(8,128)(2,1)S(1)}, bf16[512,128]{1,0:T(8,128)(2,1)S(1)}, u32[]{:S(2)}, u32[]{:S(2)}) %collective-permute-start.20) | collective-permute-done | bytes 131104 | tf_op jit(solution)/shard_map/ppermute | solution.py:301
  93.7 1.2 %shard_map.81 = bf16[512,512]{1,0:T(8,128)(2,1)} custom-call(bf16[1024,256]{1,0:T(8,128)(2,1)S(1)} %collective-permute-done.refs_1_.refs_0_, bf16[1024,256]{1,0:T(8,128)(2,1)S(1)} %collective-permute-done.1.refs_2_.refs_1_, bf16[512,128]{1,0:T(8,128)(2,1)S(1)} %collective-permute-done.18.refs_2_, bf16[512,128]{1,0:T(8,128)(2,1)S(1)} %collective-permute-done.19.refs_3_, ...), custom_call_target="tpu_custom_call" | custom-call | flops 268435456 | bytes 3145728 | tf_op jit(solution)/shard_map/pallas_call | solution.py:55
  (31 shorter events, 0.1 us)
Async XLA Ops:
  0.0 15.4 %collective-permute-start.3 = (bf16[512,512]{1,0:T(8,128)(2,1)}, bf16[512,512]{1,0:T(8,128)(2,1)S(1)}, u32[]{:S(2)}, u32[]{:S(2)}) collective-permute-start(bf16[512,512]{1,0:T(8,128)(2,1)} %refs_0_.9), channel_id=1, source_target_pairs={{0,1},{1,0},{2,3},{3,2},{4,5},{5,4},{6,7},{7,6},{8,9},{9,8},{10,11... | collective-permute-start | bytes 1572872 | tf_op jit(solution)/shard_map/ppermute | solution.py:264
  2.1 16.8 %collective-permute-start.2 = (bf16[512,512]{1,0:T(8,128)(2,1)}, bf16[512,512]{1,0:T(8,128)(2,1)}, u32[]{:S(2)}, u32[]{:S(2)}) collective-permute-start(bf16[512,512]{1,0:T(8,128)(2,1)} %refs_0_.9), channel_id=1, source_target_pairs={{0,2},{2,0},{4,6},{6,4},{1,3},{3,1},{5,7},{7,5},{8,10},{10,8},{12,... | collective-permute-start | bytes 1572872 | tf_op jit(solution)/shard_map/ppermute | solution.py:263
  3.7 6.0 %copy-start = (bf16[512,1024]{1,0:T(8,128)(2,1)S(1)}, bf16[512,1024]{1,0:T(8,128)(2,1)}, u32[]{:S(2)}) copy-start(bf16[512,1024]{1,0:T(8,128)(2,1)} %k_ref.13) | copy-start | bytes 3145732
  3.7 6.0 %copy-start.1 = (bf16[512,1024]{1,0:T(8,128)(2,1)S(1)}, bf16[512,1024]{1,0:T(8,128)(2,1)}, u32[]{:S(2)}) copy-start(bf16[512,1024]{1,0:T(8,128)(2,1)} %v_ref.13) | copy-start | bytes 3145732
  3.7 6.0 %copy-start.5 = (f32[512]{0:T(512)S(1)}, f32[512]{0:T(512)}, u32[]{:S(2)}) copy-start(f32[512]{0:T(512)} %param.7) | copy-start | bytes 6148
  7.4 8.0 %copy-start.2 = (bf16[512,1024]{1,0:T(8,128)(2,1)S(1)}, bf16[512,1024]{1,0:T(8,128)(2,1)}, u32[]{:S(2)}) copy-start(bf16[512,1024]{1,0:T(8,128)(2,1)} %q_ref.11) | copy-start | bytes 3145732
  7.4 16.3 %collective-permute-start.6 = (bf16[512,512]{1,0:T(8,128)(2,1)}, bf16[512,512]{1,0:T(8,128)(2,1)S(1)}, u32[]{:S(2)}, u32[]{:S(2)}) collective-permute-start(bf16[512,512]{1,0:T(8,128)(2,1)} %shard_map.64), channel_id=1, source_target_pairs={{2,4},{4,2},{6,0},{0,6},{3,5},{5,3},{7,1},{1,7},{10,12},{12,10},{1... | collective-permute-start | bytes 1572872 | tf_op jit(solution)/shard_map/ppermute | solution.py:266
  10.1 18.3 %collective-permute-start.11 = (bf16[512,512]{1,0:T(8,128)(2,1)S(1)}, bf16[512,512]{1,0:T(8,128)(2,1)S(1)}, u32[]{:S(2)}, u32[]{:S(2)}) collective-permute-start(bf16[512,512]{1,0:T(8,128)(2,1)S(1)} %get-tuple-element.13), channel_id=1, source_target_pairs={{0,2},{2,0},{4,6},{6,4},{1,3},{3,1},{5,7},{7,5},{8,10},{10,8},{12,... | collective-permute-start | bytes 1572872 | tf_op jit(solution)/shard_map/ppermute | solution.py:275
  10.8 10.2 %copy-start.4 = (bf16[1024,512]{1,0:T(8,128)(2,1)S(1)}, bf16[1024,512]{1,0:T(8,128)(2,1)}, u32[]{:S(2)}) copy-start(bf16[1024,512]{1,0:T(8,128)(2,1)} %refs_0_.11) | copy-start | bytes 3145732
  10.9 28.1 %collective-permute-start.14 = (bf16[512,256]{1,0:T(8,128)(2,1)S(1)}, bf16[512,256]{1,0:T(8,128)(2,1)S(1)}, u32[]{:S(2)}, u32[]{:S(2)}) collective-permute-start(bf16[512,256]{1,0:T(8,128)(2,1)S(1)} %get-tuple-element.14), channel_id=1, source_target_pairs={{0,2},{2,0},{4,6},{6,4},{1,3},{3,1},{5,7},{7,5},{8,10},{10,8},{12,... | collective-permute-start | bytes 786440 | tf_op jit(solution)/shard_map/ppermute | solution.py:276
  15.8 5.3 %copy-start.3 = (bf16[512,512]{1,0:T(8,128)(2,1)S(1)}, bf16[512,512]{1,0:T(8,128)(2,1)}, u32[]{:S(2)}) copy-start(bf16[512,512]{1,0:T(8,128)(2,1)} %refs_0_.9) | copy-start | bytes 1572868
  15.9 20.3 %collective-permute-start.8 = (bf16[512,512]{1,0:T(8,128)(2,1)S(1)}, bf16[512,512]{1,0:T(8,128)(2,1)S(1)}, u32[]{:S(2)}, u32[]{:S(2)}) collective-permute-start(bf16[512,512]{1,0:T(8,128)(2,1)S(1)} %shard_map.67), channel_id=1, source_target_pairs={{2,4},{4,2},{6,0},{0,6},{3,5},{5,3},{7,1},{1,7},{10,12},{12,10},{1... | collective-permute-start | bytes 1572872 | tf_op jit(solution)/shard_map/ppermute | solution.py:268
  19.0 17.8 %collective-permute-start.4 = (bf16[512,512]{1,0:T(8,128)(2,1)}, bf16[512,512]{1,0:T(8,128)(2,1)S(1)}, u32[]{:S(2)}, u32[]{:S(2)}) collective-permute-start(bf16[512,512]{1,0:T(8,128)(2,1)} %collective-permute-done.2.refs_1_), channel_id=1, source_target_pairs={{0,1},{1,0},{2,3},{3,2},{4,5},{5,4},{6,7},{7,6},{8,9},{9,8},{10,11... | collective-permute-start | bytes 1572872 | tf_op jit(solution)/shard_map/ppermute | solution.py:278
  24.1 19.5 %collective-permute-start.7 = (bf16[512,256]{1,0:T(8,128)(2,1)S(1)}, bf16[512,256]{1,0:T(8,128)(2,1)S(1)}, u32[]{:S(2)}, u32[]{:S(2)}) collective-permute-start(bf16[512,256]{1,0:T(8,128)(2,1)S(1)} %shard_map.66), channel_id=1, source_target_pairs={{0,2},{2,0},{4,6},{6,4},{1,3},{3,1},{5,7},{7,5},{8,10},{10,8},{12,... | collective-permute-start | bytes 786440 | tf_op jit(solution)/shard_map/ppermute | solution.py:269
  29.9 14.5 %collective-permute-start.15 = (bf16[512,256]{1,0:T(8,128)(2,1)S(1)}, bf16[512,256]{1,0:T(8,128)(2,1)S(1)}, u32[]{:S(2)}, u32[]{:S(2)}) collective-permute-start(bf16[512,256]{1,0:T(8,128)(2,1)S(1)} %shard_map.75), channel_id=1, source_target_pairs={{2,4},{4,2},{6,0},{0,6},{3,5},{5,3},{7,1},{1,7},{10,12},{12,10},{1... | collective-permute-start | bytes 786440 | tf_op jit(solution)/shard_map/ppermute | solution.py:285
  36.5 11.3 %collective-permute-start.9 = (bf16[512,256]{1,0:T(8,128)(2,1)S(1)}, bf16[512,256]{1,0:T(8,128)(2,1)S(1)}, u32[]{:S(2)}, u32[]{:S(2)}) collective-permute-start(bf16[512,256]{1,0:T(8,128)(2,1)S(1)} %shard_map.69), channel_id=1, source_target_pairs={{0,2},{2,0},{4,6},{6,4},{1,3},{3,1},{5,7},{7,5},{8,10},{10,8},{12,... | collective-permute-start | bytes 786440 | tf_op jit(solution)/shard_map/ppermute | solution.py:270
  37.2 11.3 %collective-permute-start.16 = (bf16[512,256]{1,0:T(8,128)(2,1)S(1)}, bf16[512,256]{1,0:T(8,128)(2,1)S(1)}, u32[]{:S(2)}, u32[]{:S(2)}) collective-permute-start(bf16[512,256]{1,0:T(8,128)(2,1)S(1)} %shard_map.76), channel_id=1, source_target_pairs={{2,4},{4,2},{6,0},{0,6},{3,5},{5,3},{7,1},{1,7},{10,12},{12,10},{1... | collective-permute-start | bytes 786440 | tf_op jit(solution)/shard_map/ppermute | solution.py:285
  39.0 6.7 %collective-permute-start.5 = (f32[1024]{0:T(1024)S(1)}, f32[1024]{0:T(1024)S(1)}, u32[]{:S(2)}, u32[]{:S(2)}) collective-permute-start(f32[1024]{0:T(1024)S(1)} %pad_maximum_fusion), channel_id=1, source_target_pairs={{2,4},{4,2},{6,0},{0,6},{3,5},{5,3},{7,1},{1,7},{10,12},{12,10},{1... | collective-permute-start | bytes 12296 | tf_op jit(solution)/shard_map/ppermute | solution.py:297
  43.5 9.8 %collective-permute-start.10 = (bf16[512,256]{1,0:T(8,128)(2,1)S(1)}, bf16[512,256]{1,0:T(8,128)(2,1)S(1)}, u32[]{:S(2)}, u32[]{:S(2)}) collective-permute-start(bf16[512,256]{1,0:T(8,128)(2,1)S(1)} %get-tuple-element.12), channel_id=1, source_target_pairs={{0,2},{2,0},{4,6},{6,4},{1,3},{3,1},{5,7},{7,5},{8,10},{10,8},{12,... | collective-permute-start | bytes 786440 | tf_op jit(solution)/shard_map/ppermute | solution.py:277
  44.3 29.5 %collective-permute-start.1 = (bf16[1024,256]{1,0:T(8,128)(2,1)S(1)}, bf16[1024,256]{1,0:T(8,128)(2,1)S(1)}, u32[]{:S(2)}, u32[]{:S(2)}) collective-permute-start(bf16[1024,256]{1,0:T(8,128)(2,1)S(1)} %get-tuple-element.19), channel_id=1, source_target_pairs={{0,1},{1,0},{2,3},{3,2},{4,5},{5,4},{6,7},{7,6},{8,9},{9,8},{10,11... | collective-permute-start | bytes 1572872 | tf_op jit(solution)/shard_map/ppermute | solution.py:314
  45.7 30.4 %collective-permute-start = (bf16[1024,256]{1,0:T(8,128)(2,1)S(1)}, bf16[1024,256]{1,0:T(8,128)(2,1)S(1)}, u32[]{:S(2)}, u32[]{:S(2)}) collective-permute-start(bf16[1024,256]{1,0:T(8,128)(2,1)S(1)} %get-tuple-element.20), channel_id=1, source_target_pairs={{0,1},{1,0},{2,3},{3,2},{4,5},{5,4},{6,7},{7,6},{8,9},{9,8},{10,11... | collective-permute-start | bytes 1572872 | tf_op jit(solution)/shard_map/ppermute | solution.py:314
  47.9 8.8 %collective-permute-start.12 = (bf16[512,256]{1,0:T(8,128)(2,1)S(1)}, bf16[512,256]{1,0:T(8,128)(2,1)S(1)}, u32[]{:S(2)}, u32[]{:S(2)}) collective-permute-start(bf16[512,256]{1,0:T(8,128)(2,1)S(1)} %shard_map.72), channel_id=1, source_target_pairs={{2,4},{4,2},{6,0},{0,6},{3,5},{5,3},{7,1},{1,7},{10,12},{12,10},{1... | collective-permute-start | bytes 786440 | tf_op jit(solution)/shard_map/ppermute | solution.py:285
  48.5 12.6 %collective-permute-start.13 = (bf16[512,256]{1,0:T(8,128)(2,1)S(1)}, bf16[512,256]{1,0:T(8,128)(2,1)S(1)}, u32[]{:S(2)}, u32[]{:S(2)}) collective-permute-start(bf16[512,256]{1,0:T(8,128)(2,1)S(1)} %shard_map.73), channel_id=1, source_target_pairs={{2,4},{4,2},{6,0},{0,6},{3,5},{5,3},{7,1},{1,7},{10,12},{12,10},{1... | collective-permute-start | bytes 786440 | tf_op jit(solution)/shard_map/ppermute | solution.py:285
  53.4 16.2 %collective-permute-start.17 = (bf16[512,128]{1,0:T(8,128)(2,1)S(1)}, bf16[512,128]{1,0:T(8,128)(2,1)S(1)}, u32[]{:S(2)}, u32[]{:S(2)}) collective-permute-start(bf16[512,128]{1,0:T(8,128)(2,1)S(1)} %get-tuple-element.15), channel_id=1, source_target_pairs={{0,1},{1,0},{2,3},{3,2},{4,5},{5,4},{6,7},{7,6},{8,9},{9,8},{10,11... | collective-permute-start | bytes 393224 | tf_op jit(solution)/shard_map/ppermute | solution.py:305
  56.6 19.5 %collective-permute-start.27 = (bf16[512,128]{1,0:T(8,128)(2,1)S(1)}, bf16[512,128]{1,0:T(8,128)(2,1)S(1)}, u32[]{:S(2)}, u32[]{:S(2)}) collective-permute-start(bf16[512,128]{1,0:T(8,128)(2,1)S(1)} %get-tuple-element.18.refs_1_), channel_id=1, source_target_pairs={{0,4},{2,6},{4,0},{6,2},{1,5},{3,7},{5,1},{7,3},{8,12},{10,14},{12... | collective-permute-start | bytes 393224 | tf_op jit(solution)/shard_map/ppermute | solution.py:301
  61.1 16.6 %collective-permute-start.26 = (bf16[512,128]{1,0:T(8,128)(2,1)S(1)}, bf16[512,128]{1,0:T(8,128)(2,1)S(1)}, u32[]{:S(2)}, u32[]{:S(2)}) collective-permute-start(bf16[512,128]{1,0:T(8,128)(2,1)S(1)} %get-tuple-element.18.refs_1_), channel_id=1, source_target_pairs={{2,4},{4,2},{6,0},{0,6},{3,5},{5,3},{7,1},{1,7},{10,12},{12,10},{1... | collective-permute-start | bytes 393224 | tf_op jit(solution)/shard_map/ppermute | solution.py:301
  71.9 16.7 %collective-permute-start.24 = (bf16[512,256]{1,0:T(8,128)(2,1)S(1)}, bf16[512,256]{1,0:T(8,128)(2,1)S(1)}, u32[]{:S(2)}, u32[]{:S(2)}) collective-permute-start(bf16[512,256]{1,0:T(8,128)(2,1)S(1)} %get-tuple-element.17.refs_3_.refs_7_), channel_id=1, source_target_pairs={{0,4},{2,6},{4,0},{6,2},{1,5},{3,7},{5,1},{7,3},{8,12},{10,14},{12... | collective-permute-start | bytes 786440 | tf_op jit(solution)/shard_map/ppermute | solution.py:301
  73.8 16.9 %collective-permute-start.23 = (bf16[512,256]{1,0:T(8,128)(2,1)S(1)}, bf16[512,256]{1,0:T(8,128)(2,1)S(1)}, u32[]{:S(2)}, u32[]{:S(2)}) collective-permute-start(bf16[512,256]{1,0:T(8,128)(2,1)S(1)} %get-tuple-element.17.refs_3_.refs_7_), channel_id=1, source_target_pairs={{2,4},{4,2},{6,0},{0,6},{3,5},{5,3},{7,1},{1,7},{10,12},{12,10},{1... | collective-permute-start | bytes 786440 | tf_op jit(solution)/shard_map/ppermute | solution.py:301
  76.2 14.6 %collective-permute-start.22 = (bf16[512,256]{1,0:T(8,128)(2,1)S(1)}, bf16[512,256]{1,0:T(8,128)(2,1)S(1)}, u32[]{:S(2)}, u32[]{:S(2)}) collective-permute-start(bf16[512,256]{1,0:T(8,128)(2,1)S(1)} %get-tuple-element.17.refs_3_.refs_7_), channel_id=1, source_target_pairs={{0,2},{2,0},{4,6},{6,4},{1,3},{3,1},{5,7},{7,5},{8,10},{10,8},{12,... | collective-permute-start | bytes 786440 | tf_op jit(solution)/shard_map/ppermute | solution.py:301
  76.2 6.6 %collective-permute-start.18 = (bf16[512,128]{1,0:T(8,128)(2,1)S(1)}, bf16[512,128]{1,0:T(8,128)(2,1)S(1)}, u32[]{:S(2)}, u32[]{:S(2)}) collective-permute-start(bf16[512,128]{1,0:T(8,128)(2,1)S(1)} %get-tuple-element.16), channel_id=1, source_target_pairs={{0,1},{1,0},{2,3},{3,2},{4,5},{5,4},{6,7},{7,6},{8,9},{9,8},{10,11... | collective-permute-start | bytes 393224 | tf_op jit(solution)/shard_map/ppermute | solution.py:308
  77.7 9.8 %collective-permute-start.25 = (bf16[512,128]{1,0:T(8,128)(2,1)S(1)}, bf16[512,128]{1,0:T(8,128)(2,1)S(1)}, u32[]{:S(2)}, u32[]{:S(2)}) collective-permute-start(bf16[512,128]{1,0:T(8,128)(2,1)S(1)} %get-tuple-element.18.refs_1_), channel_id=1, source_target_pairs={{0,2},{2,0},{4,6},{6,4},{1,3},{3,1},{5,7},{7,5},{8,10},{10,8},{12,... | collective-permute-start | bytes 393224 | tf_op jit(solution)/shard_map/ppermute | solution.py:301
  82.7 8.8 %collective-permute-start.21 = (bf16[512,128]{1,0:T(8,128)(2,1)S(1)}, bf16[512,128]{1,0:T(8,128)(2,1)S(1)}, u32[]{:S(2)}, u32[]{:S(2)}) collective-permute-start(bf16[512,128]{1,0:T(8,128)(2,1)S(1)} %collective-permute-done.18.refs_2_), channel_id=1, source_target_pairs={{0,4},{2,6},{4,0},{6,2},{1,5},{3,7},{5,1},{7,3},{8,12},{10,14},{12... | collective-permute-start | bytes 393224 | tf_op jit(solution)/shard_map/ppermute | solution.py:301
  87.5 6.2 %collective-permute-start.20 = (bf16[512,128]{1,0:T(8,128)(2,1)S(1)}, bf16[512,128]{1,0:T(8,128)(2,1)S(1)}, u32[]{:S(2)}, u32[]{:S(2)}) collective-permute-start(bf16[512,128]{1,0:T(8,128)(2,1)S(1)} %collective-permute-done.18.refs_2_), channel_id=1, source_target_pairs={{2,4},{4,2},{6,0},{0,6},{3,5},{5,3},{7,1},{1,7},{10,12},{12,10},{1... | collective-permute-start | bytes 393224 | tf_op jit(solution)/shard_map/ppermute | solution.py:301
  88.6 5.1 %collective-permute-start.19 = (bf16[512,128]{1,0:T(8,128)(2,1)S(1)}, bf16[512,128]{1,0:T(8,128)(2,1)S(1)}, u32[]{:S(2)}, u32[]{:S(2)}) collective-permute-start(bf16[512,128]{1,0:T(8,128)(2,1)S(1)} %collective-permute-done.18.refs_2_), channel_id=1, source_target_pairs={{0,2},{2,0},{4,6},{6,4},{1,3},{3,1},{5,7},{7,5},{8,10},{10,8},{12,... | collective-permute-start | bytes 393224 | tf_op jit(solution)/shard_map/ppermute | solution.py:301

commit v2 on v1

--- a/solution.py
+++ b/solution.py
@@ -16,7 +16,8 @@
 OPP = [(0, 2), (1, 3), (2, 0), (3, 1)]
 COL = [(0, 1), (1, 0)]
 LOG2E = 1.4426950408889634
-FIRST_MIB = 61
+FIRST_MIB = 63
+SUM_ROWS = 16
 
 
 def ring():
@@ -110,22 +111,19 @@
 def folded(gain, k_weight, v_weight):
     width = k_weight.shape[0]
 
-    def body(gain_ref, k_ref, v_ref, pass_ref, stay0_ref, stay1_ref):
+    def body(gain_ref, k_ref, v_ref, pass_ref, stay_ref):
         place = ring()
         factor = jnp.broadcast_to(gain_ref[...], (HEAD_DIM, width)).T
         for head in range(2):
             for which, ref in enumerate((k_ref, v_ref)):
-                for target, out_ref, start in (
-                    (ACROSS, pass_ref, head * PAIR),
-                    (FIRST, (stay0_ref, stay1_ref)[head], 0),
-                ):
+                start = head * PAIR + which * HEAD_DIM
+                for target, out_ref in ((ACROSS, pass_ref), (FIRST, stay_ref)):
                     block = columns_of(ref, PAIR * place[target] + head * HEAD_DIM, HEAD_DIM)
-                    start = start + which * HEAD_DIM
                     out_ref[:, start : start + HEAD_DIM] = (block.astype(F32) * factor).astype(BF16)
 
     return local_call(
         body,
-        [((width, 2 * PAIR), BF16), ((width, PAIR), BF16), ((width, PAIR), BF16)],
+        [((width, 2 * PAIR), BF16), ((width, 2 * PAIR), BF16)],
         (gain, k_weight, v_weight),
         8 * width * PAIR,
     )
@@ -152,8 +150,18 @@
     )
 
 
-def keys_values(head, target, place_of_head, pairs, gain, k_weight, v_weight, arrived, out_dtype):
+def squares(ref):
+    wide = ref[...].astype(F32)
+    return jnp.sum(wide * wide, axis=1, keepdims=True)
+
+
+def as_row(column):
+    return jnp.broadcast_to(column, (column.shape[0], HEAD_DIM)).T[:1, :]
+
+
+def keys_values(head, target, place_of_head, pairs, gain, k_weight, v_weight, arrived, out_dtype, sums):
     tokens, width = pairs[0][0].shape
+    count = tokens * len(pairs)
 
     def body(gain_ref, k_ref, v_ref, arrived_ref, *refs):
         start = PAIR * ring()[target] + head * HEAD_DIM
@@ -161,40 +169,73 @@
             [columns_of(k_ref, start, HEAD_DIM), columns_of(v_ref, start, HEAD_DIM)], axis=1
         )
         there = arrived_ref[:, place_of_head * PAIR : (place_of_head + 1) * PAIR]
+        out_ref = refs[2 * len(pairs)]
+        rows = []
         for index in range(len(pairs)):
-            value = dot(gained(refs[2 * index], gain_ref), weight) + dot(refs[2 * index + 1][...], there)
-            refs[-1][index * tokens : (index + 1) * tokens, :] = value.astype(out_dtype)
-
-    return local_call(
-        body,
-        [((tokens * len(pairs), PAIR), out_dtype)],
+            near_ref, far_ref = refs[2 * index], refs[2 * index + 1]
+            value = dot(gained(near_ref, gain_ref), weight) + dot(far_ref[...], there)
+            out_ref[index * tokens : (index + 1) * tokens, :] = value.astype(out_dtype)
+            if sums:
+                row = as_row(squares(near_ref) + squares(far_ref))
+                refs[-1][:, index * tokens : (index + 1) * tokens] = row
+                rows += [row[:, cut : cut + PAIR] for cut in range(0, tokens, PAIR)]
+        if sums:
+            rest = jnp.concatenate(rows, axis=0)
+            terms = []
+            for _ in range(3):
+                terms.append(rest.astype(BF16))
+                rest = rest - terms[-1].astype(F32)
+            blank = jnp.zeros((SUM_ROWS - 3 * len(rows), PAIR), F32)
+            wide = [term.astype(F32) for term in terms] + [blank]
+            out_ref[count:, :] = jnp.concatenate(wide, axis=0).astype(out_dtype)
+
+    shapes = [((count + (SUM_ROWS if sums else 0), PAIR), out_dtype)]
+    if sums:
+        shapes.append(((1, count), F32))
+    return local_call(
+        body,
+        shapes,
         (gain, k_weight, v_weight, arrived, *[block for pair in pairs for block in pair]),
         4 * tokens * width * PAIR * len(pairs),
     )
 
 
-def attend(head, q_own, q_other, kept, far_own, far_other, scale, beside):
-    half = far_own.shape[0]
-    block = 256
+def attend(head, q_kept, q_end, kept, far, near_sums, far_sums, beside):
+    count = kept.shape[0]
+    half = count // 2
+    block = 512
     offset = 0 if beside is None else HEAD_DIM
-    operands = [scale, *q_own, *q_other, kept, far_own, far_other]
-    operands += [] if beside is None else [beside]
-
-    def body(scale_ref, qa_ref, qb_ref, qc_ref, qd_ref, kept_ref, own_ref, other_ref, *refs):
-        out_other_ref, out_own_ref, q_ref, k_ref, v_ref = refs[-5:]
-        if beside is not None:
-            out_own_ref[:, :HEAD_DIM] = refs[0][...]
+    groups = [q_kept, q_end, far, near_sums, far_sums, [kept], [] if beside is None else [beside]]
+    operands = [x for group in groups for x in group]
+
+    def body(*refs):
+        refs = list(refs)
+        qk_refs, qe_refs, far_refs, near_sums_refs, far_sums_refs, (kept_ref,), beside_refs = [
+            [refs.pop(0) for _ in group] for group in groups
+        ]
+        out_other_ref, out_own_ref, q_ref, k_ref, v_ref = refs
+        if beside_refs:
+            out_own_ref[:, :HEAD_DIM] = beside_refs[0][...]
         cut = slice(head * HEAD_DIM, (head + 1) * HEAD_DIM)
-        for index, (first_ref, second_ref, far_ref) in enumerate(
-            ((qa_ref, qb_ref, own_ref), (qc_ref, qd_ref, other_ref))
-        ):
-            rows = slice(index * half, (index + 1) * half)
-            factor = jnp.broadcast_to(scale_ref[:, rows], (HEAD_DIM, half)).T
-            query = first_ref[:, cut].astype(F32) + second_ref[:, cut].astype(F32)
-            value = kept_ref[rows, :] + far_ref[...].astype(F32)
-            q_ref[rows, :] = (query * (factor * (LOG2E / HEAD_DIM**0.5))).astype(BF16)
-            k_ref[rows, :] = (value[:, :HEAD_DIM] * factor).astype(BF16)
-            v_ref[rows, :] = (value[:, HEAD_DIM:] * factor).astype(BF16)
+        lines = half // PAIR
+        for index in range(2):
+            coded = far_sums_refs[index][half : half + SUM_ROWS, :].astype(F32)
+            sums = coded[:lines, :] + coded[lines : 2 * lines, :] + coded[2 * lines : 3 * lines, :]
+            for part in range(lines):
+                near = slice(part * PAIR, (part + 1) * PAIR)
+                rows = slice(index * half + part * PAIR, index * half + (part + 1) * PAIR)
+                total = near_sums_refs[index][:, near] + sums[part : part + 1, :]
+                scale = lax.rsqrt(total / D + 1e-06)
+                factor = jnp.broadcast_to(scale, (HEAD_DIM, PAIR)).T
+                query = qk_refs[index][near, cut].astype(F32) + qe_refs[index][near, cut].astype(F32)
+                if len(far_refs) == 2:
+                    arrived = far_refs[index][near, :]
+                else:
+                    arrived = far_refs[0][rows, :]
+                value = kept_ref[rows, :] + arrived.astype(F32)
+                q_ref[rows, :] = (query * (factor * (LOG2E / HEAD_DIM**0.5))).astype(BF16)
+                k_ref[rows, :] = (value[:, :HEAD_DIM] * factor).astype(BF16)
+                v_ref[rows, :] = (value[:, HEAD_DIM:] * factor).astype(BF16)
         for start in list(range(half, 2 * half, block)) + list(range(0, half, block)):
             scores = lax.dot_general(
                 q_ref[start : start + block, :],
@@ -216,7 +257,7 @@
         operands,
         16 * half * half * HEAD_DIM,
         14,
-        scratch=[pltpu.VMEM((2 * half, HEAD_DIM), BF16)] * 3,
+        scratch=[pltpu.VMEM((count, HEAD_DIM), BF16)] * 3,
         exps=4 * half * half,
     )
 
@@ -253,7 +294,11 @@
         refs[-1][...] = total.astype(out_dtype)
 
     return local_call(
-        body, [((tokens, columns), out_dtype)], operands, 2 * tokens * columns * HEAD_DIM * len(terms), 12
+        body,
+        [((tokens, columns), out_dtype)],
+        operands,
+        2 * tokens * columns * HEAD_DIM * len(terms),
+        12,
     )
 
 
@@ -267,51 +312,52 @@
     both = (ACROSS, SECOND)
     q_other = lax.ppermute(queries(both, other, gain, q_weight, None, BF16), "row", P2)
     end_own = lax.ppermute(queries((FIRST,), own, gain, q_weight, (q_own, 0), BF16), "row", P1)
-    end_other = lax.ppermute(queries((FIRST,), other, gain, q_weight, (q_other, 0), BF16), "row", P1)
+    end_other = lax.ppermute(
+        queries((FIRST,), other, gain, q_weight, (q_other, 0), BF16), "row", P1
+    )
     kept_q_own = queries((ME,), own, gain, q_weight, (q_own, 1), F32)
     kept_q_other = queries((ME,), other, gain, q_weight, (q_other, 1), F32)
 
-    pass_block, stay_block0, stay_block1 = folded(gain, k_weight, v_weight)
+    pass_block, stay_block = folded(gain, k_weight, v_weight)
     passed = lax.ppermute(pass_block, "row", P1)
-    stay0 = lax.ppermute(stay_block0, "row", P1)
-    stay1 = lax.ppermute(stay_block1, "row", P1)
+    stay = lax.ppermute(stay_block, "row", P1)
     other1 = lax.ppermute(own1, "col", COL)
-
-    def partial(head, target, place, pairs, arrived, out_dtype):
-        return keys_values(head, target, place, pairs, gain, k_weight, v_weight, arrived, out_dtype)
-
-    def sent_partial(head, pair):
-        value = partial(head, SECOND, head, [pair], passed, BF16)
-        return lax.ppermute(value, "row", P2)
-
-    far0_own = sent_partial(0, (own, own1))
-    far0_other = sent_partial(0, (other, other1))
-    far1_own = sent_partial(1, (own, own1))
-    far1_other = sent_partial(1, (other, other1))
-    all_pairs = [(own, own1), (other, other1)]
-    kept0 = partial(0, ME, 0, all_pairs, stay0, F32)
-    kept1 = partial(1, ME, 0, all_pairs, stay1, F32)
-
-    square = lambda x: jnp.sum(jnp.square(x.astype(F32)), axis=1)
-    total = jnp.concatenate([square(own) + square(own1), square(other) + square(other1)])
-    total = total + lax.ppermute(total, "row", P2)
-    scale = lax.rsqrt(total / D + 1e-06)[None, :]
+    pairs = [(own, own1), (other, other1)]
+
+    def partial(head, target, place, pairs, arrived, out_dtype, sums=False):
+        return keys_values(
+            head, target, place, pairs, gain, k_weight, v_weight, arrived, out_dtype, sums
+        )
+
+    value, sums_own = partial(0, SECOND, 0, pairs[:1], passed, BF16, True)
+    far0_own = lax.ppermute(value, "row", P2)
+    value, sums_other = partial(0, SECOND, 0, pairs[1:], passed, BF16, True)
+    far0_other = lax.ppermute(value, "row", P2)
+    far0 = [far0_own, far0_other]
+    far1 = [lax.ppermute(partial(1, SECOND, 1, pairs, passed, BF16), "row", P2)]
+    near_sums = [sums_own, sums_other]
+    kept0 = partial(0, ME, 0, pairs, stay, F32)
+    kept1 = partial(1, ME, 1, pairs, stay, F32)
 
     def from_all(value):
-        return [value, lax.ppermute(value, "row", P1), lax.ppermute(value, "row", P2), lax.ppermute(value, "row", OPP)]
-
-    q_parts = ((kept_q_own, end_own), (kept_q_other, end_other))
-    other0, own0 = attend(0, *q_parts, kept0, far0_own, far0_other, scale, None)
+        return [
+            value,
+            lax.ppermute(value, "row", P1),
+            lax.ppermute(value, "row", P2),
+            lax.ppermute(value, "row", OPP),
+        ]
+
+    q_parts = ((kept_q_own, kept_q_other), (end_own, end_other))
+    other0, own0 = attend(0, *q_parts, kept0, far0, near_sums, far0, None)
     partner0 = lax.ppermute(other0, "col", COL)
     own0_all = from_all(own0)
-    other1_mixed, middle = attend(1, *q_parts, kept1, far1_own, far1_other, scale, partner0)
+    other1_mixed, middle = attend(1, *q_parts, kept1, far1, near_sums, far0, partner0)
     partner1 = lax.ppermute(other1_mixed, "col", COL)
     middle_all = from_all(middle)
     partner1_all = from_all(partner1)
 
-    half = out_weight.shape[1] // 2
     here = [out_weight]
-    there = [lax.ppermute(out_weight[:, :half], "col", COL), lax.ppermute(out_weight[:, half:], "col", COL)]
+    there = [lax.ppermute(out_weight, "col", COL)]
     terms = [(x, 0, 0, 0, source) for source, x in enumerate(own0_all)]
     total = output_product(terms, [here], None, F32)
     terms = [(x, 0, 1, 0, source) for source, x in enumerate(middle_all)]

time: 96.2 us -> 92.7 us (0.964)
  starting transfers between devices: 46.6 us -> 42.1 us
  local copies, waits for them, and re-layouts: 0.1 us -> 2.48 us
  other arithmetic: 1.78 us -> 0 us
    ppermute x9 -> x5, waiting for transfers between devices: 3.73 us -> 10.1 us  [the longest x1 7.16 us: sublayer(): far0_own = lax.ppermute(value, 'row', P2)]
    ppermute x1, waiting for transfers between devices: 4.79 us -> 0.01 us  [sublayer(): partner0 = lax.ppermute(other0, 'col', COL)]
    ppermute x9 -> x5, starting transfers between devices: 15.6 us -> 11.2 us  [the longest x1 4.23 us: sublayer(): far1 = [lax.ppermute(partial(1, SECOND, 1, pairs, passed, BF16), 'row', P2)]]
    ppermute x3, starting transfers between devices: 4.92 us -> 9.16 us  [from_all(): lax.ppermute(value, 'row', OPP)]
    ppermute x3, starting transfers between devices: 7.17 us -> 3.15 us  [from_all(): lax.ppermute(value, 'row', P2)]
    ppermute x1, waiting for transfers between devices: 3.18 us -> 0.01 us  [sublayer(): other = lax.ppermute(own, 'col', COL)]
    ppermute x1, waiting for transfers between devices: 0.01 us -> 2.49 us  [sublayer(): other1 = lax.ppermute(own1, 'col', COL)]
    unnamed x12 -> x16, local copies, waits for them, and re-layouts: 0.03 us -> 2.48 us
  transfers between devices with their start and end apart: 28 -> 24, of which waited for: 8 -> 11; matrix products, arithmetic and copies ran while one was open for 2% -> 0% of each run, Pallas kernels for 20% -> 20%
where the time goes in v2:
time: 92.7 us; the launch traced here: 91.1 us
  starting transfers between devices  42.1 us (45%)
  waiting for transfers between devices  26.5 us (29%)
  Pallas kernels  19.8 us (21%)
  local copies, waits for them, and re-layouts  2.48 us (3%)
    pallas_call x17, Pallas kernels, local_call(): pl.pallas_call(body, in_specs=in_specs or [VMEM] * len(operands), out_spe...  19.8 us
    ppermute x3, starting transfers between devices, from_all(): lax.ppermute(value, 'row', OPP)  9.16 us
    ppermute x1, waiting for transfers between devices, sublayer(): far0_own = lax.ppermute(value, 'row', P2)  7.16 us
    ppermute x3, waiting for transfers between devices, from_all(): lax.ppermute(value, 'row', P2)  4.28 us
    ppermute x1, starting transfers between devices, sublayer(): far1 = [lax.ppermute(partial(1, SECOND, 1, pairs, passed, BF16), 'row', P2)]  4.23 us
    ppermute x3, starting transfers between devices, from_all(): lax.ppermute(value, 'row', P2)  3.15 us
    ppermute x1, waiting for transfers between devices, sublayer(): far0_other = lax.ppermute(value, 'row', P2)  2.89 us
    ppermute x3, waiting for transfers between devices, from_all(): lax.ppermute(value, 'row', P1)  2.61 us
  transfers between devices with their start and end apart: 24, of which 11 were waited for; matrix products, arithmetic and copies ran while one was open for 0% of the time, Pallas kernels for 20%

profile of v2, /device:TPU:130, one launch (start us, length us, event | category | flops | bytes accessed | tf_op | source)
XLA Modules:
  0.0 91.1 jit_solution(15227611291226340455)
XLA Ops:
  0.0 1.6 %collective-permute-start.7 = (bf16[512,512]{1,0:T(8,128)(2,1)}, bf16[512,512]{1,0:T(8,128)(2,1)}, u32[]{:S(2)}, u32[]{:S(2)}) collective-permute-start(bf16[512,512]{1,0:T(8,128)(2,1)} %refs_0_.9), channel_id=1, source_target_pairs={{0,2},{2,0},{4,6},{6,4},{1,3},{3,1},{5,7},{7,5},{8,10},{10,8},{12,... | collective-permute-start | bytes 1572872 | tf_op jit(solution)/shard_map/ppermute | solution.py:308
  1.6 2.1 %collective-permute-start.2 = (bf16[512,512]{1,0:T(8,128)(2,1)}, bf16[512,512]{1,0:T(8,128)(2,1)S(1)}, u32[]{:S(2)}, u32[]{:S(2)}) collective-permute-start(bf16[512,512]{1,0:T(8,128)(2,1)} %refs_0_.9), channel_id=1, source_target_pairs={{0,1},{1,0},{2,3},{3,2},{4,5},{5,4},{6,7},{7,6},{8,9},{9,8},{10,11... | collective-permute-start | bytes 1572872 | tf_op jit(solution)/shard_map/ppermute | solution.py:309
  3.7 3.6 %shard_map.64 = bf16[512,512]{1,0:T(8,128)(2,1)} custom-call(f32[1,512]{1,0:T(1,128)} %bitcast.1, bf16[512,512]{1,0:T(8,128)(2,1)} %refs_0_.9, bf16[512,1024]{1,0:T(8,128)(2,1)} %q_ref.11), custom_call_target="tpu_custom_call" | custom-call | flops 268435456 | bytes 2099200 | tf_op jit(solution)/shard_map/pallas_call | solution.py:56
  7.3 2.3 %collective-permute-start.1 = (bf16[512,512]{1,0:T(8,128)(2,1)}, bf16[512,512]{1,0:T(8,128)(2,1)S(1)}, u32[]{:S(2)}, u32[]{:S(2)}) collective-permute-start(bf16[512,512]{1,0:T(8,128)(2,1)} %shard_map.64), channel_id=1, source_target_pairs={{2,4},{4,2},{6,0},{0,6},{3,5},{5,3},{7,1},{1,7},{10,12},{12,10},{1... | collective-permute-start | bytes 1572872 | tf_op jit(solution)/shard_map/ppermute | solution.py:311
  9.6 1.2 %copy-done = bf16[512,1024]{1,0:T(8,128)(2,1)S(1)} copy-done((bf16[512,1024]{1,0:T(8,128)(2,1)S(1)}, bf16[512,1024]{1,0:T(8,128)(2,1)}, u32[]{:S(2)}) %copy-start) | copy-done | bytes 1048600
  10.8 1.2 %copy-done.2 = bf16[512,1024]{1,0:T(8,128)(2,1)S(1)} copy-done((bf16[512,1024]{1,0:T(8,128)(2,1)S(1)}, bf16[512,1024]{1,0:T(8,128)(2,1)}, u32[]{:S(2)}) %copy-start.2) | copy-done | bytes 1048600
  12.1 0.4 shard_map.70
  12.4 0.8 collective-permute-start.6
  13.2 0.8 collective-permute-done.7.refs_1_
  14.0 2.6 %collective-permute-start.8 = (bf16[512,512]{1,0:T(8,128)(2,1)}, bf16[512,512]{1,0:T(8,128)(2,1)S(1)}, u32[]{:S(2)}, u32[]{:S(2)}) collective-permute-start(bf16[512,512]{1,0:T(8,128)(2,1)} %collective-permute-done.7.refs_1_), channel_id=1, source_target_pairs={{0,1},{1,0},{2,3},{3,2},{4,5},{5,4},{6,7},{7,6},{8,9},{9,8},{10,11... | collective-permute-start | bytes 1572872 | tf_op jit(solution)/shard_map/ppermute | solution.py:324
  16.6 2.2 %collective-permute-start.12 = (bf16[512,512]{1,0:T(8,128)(2,1)S(1)}, bf16[512,512]{1,0:T(8,128)(2,1)S(1)}, u32[]{:S(2)}, u32[]{:S(2)}) collective-permute-start(bf16[512,512]{1,0:T(8,128)(2,1)S(1)} %get-tuple-element.20), channel_id=1, source_target_pairs={{0,2},{2,0},{4,6},{6,4},{1,3},{3,1},{5,7},{7,5},{8,10},{10,8},{12,... | collective-permute-start | bytes 1572872 | tf_op jit(solution)/shard_map/ppermute | solution.py:323
  18.8 0.0 collective-permute-done.2.near_ref.refs_2_.refs_0_
  18.8 0.5 shard_map.66
  19.3 0.0 copy-start.1
  19.3 0.0 copy-start.3
  19.3 2.3 %collective-permute-start.3 = (bf16[512,512]{1,0:T(8,128)(2,1)S(1)}, bf16[512,512]{1,0:T(8,128)(2,1)S(1)}, u32[]{:S(2)}, u32[]{:S(2)}) collective-permute-start(bf16[512,512]{1,0:T(8,128)(2,1)S(1)} %shard_map.66), channel_id=1, source_target_pairs={{2,4},{4,2},{6,0},{0,6},{3,5},{5,3},{7,1},{1,7},{10,12},{12,10},{1... | collective-permute-start | bytes 1572872 | tf_op jit(solution)/shard_map/ppermute | solution.py:313
  21.6 1.8 %collective-permute-done.1.refs_0_ = bf16[512,512]{1,0:T(8,128)(2,1)S(1)} collective-permute-done((bf16[512,512]{1,0:T(8,128)(2,1)}, bf16[512,512]{1,0:T(8,128)(2,1)S(1)}, u32[]{:S(2)}, u32[]{:S(2)}) %collective-permute-start.1) | collective-permute-done | bytes 524320 | tf_op jit(solution)/shard_map/ppermute | solution.py:311
  23.4 1.4 %collective-permute-start = (bf16[1024,512]{1,0:T(8,128)(2,1)S(1)}, bf16[1024,512]{1,0:T(8,128)(2,1)S(1)}, u32[]{:S(2)}, u32[]{:S(2)}) collective-permute-start(bf16[1024,512]{1,0:T(8,128)(2,1)S(1)} %copy-done.6), channel_id=1, source_target_pairs={{0,1},{1,0},{2,3},{3,2},{4,5},{5,4},{6,7},{7,6},{8,9},{9,8},{10,11... | collective-permute-start | bytes 3145736 | tf_op jit(solution)/shard_map/ppermute | solution.py:360
  24.8 0.3 shard_map.68
  25.1 2.2 %collective-permute-done.6.arrived_ref = bf16[512,512]{1,0:T(8,128)(2,1)S(1)} collective-permute-done((bf16[512,512]{1,0:T(8,128)(2,1)S(1)}, bf16[512,512]{1,0:T(8,128)(2,1)S(1)}, u32[]{:S(2)}, u32[]{:S(2)}) %collective-permute-start.6) | collective-permute-done | bytes 524320 | tf_op jit(solution)/shard_map/ppermute | solution.py:322
  27.3 0.7 collective-permute-start.4
  28.0 2.5 %collective-permute-done.8.refs_3_.refs_1_ = bf16[512,512]{1,0:T(8,128)(2,1)S(1)} collective-permute-done((bf16[512,512]{1,0:T(8,128)(2,1)}, bf16[512,512]{1,0:T(8,128)(2,1)S(1)}, u32[]{:S(2)}, u32[]{:S(2)}) %collective-permute-start.8) | collective-permute-done | bytes 524320 | tf_op jit(solution)/shard_map/ppermute | solution.py:324
  30.5 1.8 %shard_map.71 = bf16[1024,256]{1,0:T(8,128)(2,1)S(1)} custom-call(f32[1,512]{1,0:T(1,128)S(1)} %bitcast.5, bf16[512,1024]{1,0:T(8,128)(2,1)S(1)} %copy-done.1, bf16[512,1024]{1,0:T(8,128)(2,1)S(1)} %copy-done.3, bf16[512,512]{1,0:T(8,128)(2,1)S(1)} %collective-permute-done.6.arrived_ref, bf16[512,512]{1,0:T(8,128)(2,1)S(1)} %copy-done.5, ...), custom_call_target="tpu_custom_call" | custom-call | flops 536870912 | bytes 5244928 | tf_op jit(solution)/shard_map/pallas_call | solution.py:56
  32.3 4.2 %collective-permute-start.9 = (bf16[1024,256]{1,0:T(8,128)(2,1)S(1)}, bf16[1024,256]{1,0:T(8,128)(2,1)S(1)}, u32[]{:S(2)}, u32[]{:S(2)}) collective-permute-start(bf16[1024,256]{1,0:T(8,128)(2,1)S(1)} %shard_map.71), channel_id=1, source_target_pairs={{2,4},{4,2},{6,0},{0,6},{3,5},{5,3},{7,1},{1,7},{10,12},{12,10},{1... | collective-permute-start | bytes 1572872 | tf_op jit(solution)/shard_map/ppermute | solution.py:337
  36.5 1.6 %shard_map.72 = (bf16[528,256]{1,0:T(8,128)(2,1)S(1)}, f32[1,512]{1,0:T(1,128)S(1)}) custom-call(f32[1,512]{1,0:T(1,128)S(1)} %bitcast.6, bf16[512,1024]{1,0:T(8,128)(2,1)S(1)} %copy-done.1, bf16[512,1024]{1,0:T(8,128)(2,1)S(1)} %copy-done.3, bf16[512,512]{1,0:T(8,128)(2,1)S(1)} %collective-permute-done.6.arrived_ref, bf16[512,512]{1,0:T(8,128)(2,1)S(1)} %copy-done.5, ...), custom_call_target="tpu_custom_call" | custom-call | flops 268435456 | bytes 3944448 | tf_op jit(solution)/shard_map/pallas_call | solution.py:56
  38.1 0.5 shard_map.73
  38.6 0.0 collective-permute-done.12.arrived_ref
  38.6 1.9 %collective-permute-start.10 = (bf16[528,256]{1,0:T(8,128)(2,1)S(1)}, bf16[528,256]{1,0:T(8,128)(2,1)S(1)}, u32[]{:S(2)}, u32[]{:S(2)}) collective-permute-start(bf16[528,256]{1,0:T(8,128)(2,1)S(1)} %get-tuple-element.18), channel_id=1, source_target_pairs={{2,4},{4,2},{6,0},{0,6},{3,5},{5,3},{7,1},{1,7},{10,12},{12,10},{1... | collective-permute-start | bytes 811016 | tf_op jit(solution)/shard_map/ppermute | solution.py:333
  40.5 1.4 %collective-permute-start.11 = (bf16[528,256]{1,0:T(8,128)(2,1)S(1)}, bf16[528,256]{1,0:T(8,128)(2,1)S(1)}, u32[]{:S(2)}, u32[]{:S(2)}) collective-permute-start(bf16[528,256]{1,0:T(8,128)(2,1)S(1)} %get-tuple-element.19), channel_id=1, source_target_pairs={{2,4},{4,2},{6,0},{0,6},{3,5},{5,3},{7,1},{1,7},{10,12},{12,10},{1... | collective-permute-start | bytes 811016 | tf_op jit(solution)/shard_map/ppermute | solution.py:335
  41.9 0.3 shard_map.69
  42.3 1.3 %collective-permute-start.5 = (bf16[512,256]{1,0:T(8,128)(2,1)S(1)}, bf16[512,256]{1,0:T(8,128)(2,1)S(1)}, u32[]{:S(2)}, u32[]{:S(2)}) collective-permute-start(bf16[512,256]{1,0:T(8,128)(2,1)S(1)} %shard_map.69), channel_id=1, source_target_pairs={{0,2},{2,0},{4,6},{6,4},{1,3},{3,1},{5,7},{7,5},{8,10},{10,8},{12,... | collective-permute-start | bytes 786440 | tf_op jit(solution)/shard_map/ppermute | solution.py:315
  43.5 0.3 shard_map.65.refs_0_
  43.9 0.3 shard_map.67.refs_1_
  44.2 1.8 %shard_map.75.refs_10_ = f32[1024,256]{1,0:T(8,128)S(1)} custom-call(f32[1,512]{1,0:T(1,128)S(1)} %bitcast.11, bf16[512,1024]{1,0:T(8,128)(2,1)S(1)} %copy-done.1, bf16[512,1024]{1,0:T(8,128)(2,1)S(1)} %copy-done.3, bf16[512,512]{1,0:T(8,128)(2,1)S(1)} %collective-permute-done.12.arrived_ref, bf16[512,512]{1,0:T(8,128)(2,1)S(1)} %copy-done.5, ...), custom_call_target="tpu_custom_call" | custom-call | flops 536870912 | bytes 5769216 | tf_op jit(solution)/shard_map/pallas_call | solution.py:56
  45.9 7.2 %collective-permute-done.10.refs_4_.refs_8_.refs_7_ = bf16[528,256]{1,0:T(8,128)(2,1)S(1)} collective-permute-done((bf16[528,256]{1,0:T(8,128)(2,1)S(1)}, bf16[528,256]{1,0:T(8,128)(2,1)S(1)}, u32[]{:S(2)}, u32[]{:S(2)}) %collective-permute-start.10) | collective-permute-done | bytes 270368 | tf_op jit(solution)/shard_map/ppermute | solution.py:333
  53.1 0.0 collective-permute-done.5.refs_3_
  53.1 2.9 %collective-permute-done.11.refs_5_.refs_9_.refs_8_ = bf16[528,256]{1,0:T(8,128)(2,1)S(1)} collective-permute-done((bf16[528,256]{1,0:T(8,128)(2,1)S(1)}, bf16[528,256]{1,0:T(8,128)(2,1)S(1)}, u32[]{:S(2)}, u32[]{:S(2)}) %collective-permute-start.11) | collective-permute-done | bytes 270368 | tf_op jit(solution)/shard_map/ppermute | solution.py:335
  56.0 2.2 %shard_map.76 = (bf16[512,128]{1,0:T(8,128)(2,1)S(1)}, bf16[512,128]{1,0:T(8,128)(2,1)S(1)}) custom-call(f32[512,256]{1,0:T(8,128)S(1)} %shard_map.65.refs_0_, f32[512,256]{1,0:T(8,128)S(1)} %shard_map.67.refs_1_, bf16[512,256]{1,0:T(8,128)(2,1)S(1)} %collective-permute-done.4.refs_2_, bf16[512,256]{1,0:T(8,128)(2,1)S(1)} %collective-permute-done.5.refs_3_, ...), custom_call_target="tpu_custom_call" | custom-call | flops 536870912 | bytes 3969024 | tf_op jit(solution)/shard_map/pallas_call | solution.py:56
  58.2 1.5 %collective-permute-start.13 = (bf16[512,128]{1,0:T(8,128)(2,1)S(1)}, bf16[512,128]{1,0:T(8,128)(2,1)S(1)}, u32[]{:S(2)}, u32[]{:S(2)}) collective-permute-start(bf16[512,128]{1,0:T(8,128)(2,1)S(1)} %get-tuple-element.21), channel_id=1, source_target_pairs={{0,1},{1,0},{2,3},{3,2},{4,5},{5,4},{6,7},{7,6},{8,9},{9,8},{10,11... | collective-permute-start | bytes 393224 | tf_op jit(solution)/shard_map/ppermute | solution.py:352
  59.7 1.7 %shard_map.74.refs_9_ = f32[1024,256]{1,0:T(8,128)S(1)} custom-call(f32[1,512]{1,0:T(1,128)S(1)} %bitcast.12, bf16[512,1024]{1,0:T(8,128)(2,1)S(1)} %copy-done.1, bf16[512,1024]{1,0:T(8,128)(2,1)S(1)} %copy-done.3, bf16[512,512]{1,0:T(8,128)(2,1)S(1)} %collective-permute-done.12.arrived_ref, bf16[512,512]{1,0:T(8,128)(2,1)S(1)} %copy-done.5, ...), custom_call_target="tpu_custom_call" | custom-call | flops 536870912 | bytes 5769216 | tf_op jit(solution)/shard_map/pallas_call | solution.py:56
  61.4 2.3 %collective-permute-start.23 = (bf16[512,128]{1,0:T(8,128)(2,1)S(1)}, bf16[512,128]{1,0:T(8,128)(2,1)S(1)}, u32[]{:S(2)}, u32[]{:S(2)}) collective-permute-start(bf16[512,128]{1,0:T(8,128)(2,1)S(1)} %get-tuple-element.24.refs_1_), channel_id=1, source_target_pairs={{0,4},{2,6},{4,0},{6,2},{1,5},{3,7},{5,1},{7,3},{8,12},{10,14},{12... | collective-permute-start | bytes 393224 | tf_op jit(solution)/shard_map/ppermute | solution.py:347
  63.7 1.1 %collective-permute-start.22 = (bf16[512,128]{1,0:T(8,128)(2,1)S(1)}, bf16[512,128]{1,0:T(8,128)(2,1)S(1)}, u32[]{:S(2)}, u32[]{:S(2)}) collective-permute-start(bf16[512,128]{1,0:T(8,128)(2,1)S(1)} %get-tuple-element.24.refs_1_), channel_id=1, source_target_pairs={{2,4},{4,2},{6,0},{0,6},{3,5},{5,3},{7,1},{1,7},{10,12},{12,10},{1... | collective-permute-start | bytes 393224 | tf_op jit(solution)/shard_map/ppermute | solution.py:346
  64.8 2.2 %shard_map.77 = (bf16[512,128]{1,0:T(8,128)(2,1)S(1)}, bf16[512,256]{1,0:T(8,128)(2,1)S(1)}) custom-call(f32[512,256]{1,0:T(8,128)S(1)} %shard_map.65.refs_0_, f32[512,256]{1,0:T(8,128)S(1)} %shard_map.67.refs_1_, bf16[512,256]{1,0:T(8,128)(2,1)S(1)} %collective-permute-done.4.refs_2_, bf16[512,256]{1,0:T(8,128)(2,1)S(1)} %collective-permute-done.5.refs_3_, ...), custom_call_target="tpu_custom_call" | custom-call | flops 536870912 | bytes 4214784 | tf_op jit(solution)/shard_map/pallas_call | solution.py:56
  67.0 2.9 %collective-permute-start.20 = (bf16[512,256]{1,0:T(8,128)(2,1)S(1)}, bf16[512,256]{1,0:T(8,128)(2,1)S(1)}, u32[]{:S(2)}, u32[]{:S(2)}) collective-permute-start(bf16[512,256]{1,0:T(8,128)(2,1)S(1)} %get-tuple-element.23.refs_2_.refs_6_), channel_id=1, source_target_pairs={{0,4},{2,6},{4,0},{6,2},{1,5},{3,7},{5,1},{7,3},{8,12},{10,14},{12... | collective-permute-start | bytes 786440 | tf_op jit(solution)/shard_map/ppermute | solution.py:347
  69.9 0.6 collective-permute-start.19
  70.5 0.0 collective-permute-done.refs_1_.refs_0_
  70.5 0.1 collective-permute-start.18
  70.6 0.0 collective-permute-done.23.refs_4_
  70.6 1.9 %collective-permute-start.14 = (bf16[512,128]{1,0:T(8,128)(2,1)S(1)}, bf16[512,128]{1,0:T(8,128)(2,1)S(1)}, u32[]{:S(2)}, u32[]{:S(2)}) collective-permute-start(bf16[512,128]{1,0:T(8,128)(2,1)S(1)} %get-tuple-element.22), channel_id=1, source_target_pairs={{0,1},{1,0},{2,3},{3,2},{4,5},{5,4},{6,7},{7,6},{8,9},{9,8},{10,11... | collective-permute-start | bytes 393224 | tf_op jit(solution)/shard_map/ppermute | solution.py:355
  72.5 1.5 %collective-permute-done.22.refs_3_ = bf16[512,128]{1,0:T(8,128)(2,1)S(1)} collective-permute-done((bf16[512,128]{1,0:T(8,128)(2,1)S(1)}, bf16[512,128]{1,0:T(8,128)(2,1)S(1)}, u32[]{:S(2)}, u32[]{:S(2)}) %collective-permute-start.22) | collective-permute-done | bytes 131104 | tf_op jit(solution)/shard_map/ppermute | solution.py:346
  73.9 0.9 collective-permute-start.21
  74.8 2.3 %collective-permute-done.14.refs_1_ = bf16[512,128]{1,0:T(8,128)(2,1)S(1)} collective-permute-done((bf16[512,128]{1,0:T(8,128)(2,1)S(1)}, bf16[512,128]{1,0:T(8,128)(2,1)S(1)}, u32[]{:S(2)}, u32[]{:S(2)}) %collective-permute-start.14) | collective-permute-done | bytes 131104 | tf_op jit(solution)/shard_map/ppermute | solution.py:355
  77.1 4.0 %collective-permute-start.17 = (bf16[512,128]{1,0:T(8,128)(2,1)S(1)}, bf16[512,128]{1,0:T(8,128)(2,1)S(1)}, u32[]{:S(2)}, u32[]{:S(2)}) collective-permute-start(bf16[512,128]{1,0:T(8,128)(2,1)S(1)} %collective-permute-done.14.refs_1_), channel_id=1, source_target_pairs={{0,4},{2,6},{4,0},{6,2},{1,5},{3,7},{5,1},{7,3},{8,12},{10,14},{12... | collective-permute-start | bytes 393224 | tf_op jit(solution)/shard_map/ppermute | solution.py:347
  81.1 2.4 %collective-permute-done.21.refs_2_ = bf16[512,128]{1,0:T(8,128)(2,1)S(1)} collective-permute-done((bf16[512,128]{1,0:T(8,128)(2,1)S(1)}, bf16[512,128]{1,0:T(8,128)(2,1)S(1)}, u32[]{:S(2)}, u32[]{:S(2)}) %collective-permute-start.21) | collective-permute-done | bytes 131104 | tf_op jit(solution)/shard_map/ppermute | solution.py:345
  83.5 1.4 %collective-permute-start.16 = (bf16[512,128]{1,0:T(8,128)(2,1)S(1)}, bf16[512,128]{1,0:T(8,128)(2,1)S(1)}, u32[]{:S(2)}, u32[]{:S(2)}) collective-permute-start(bf16[512,128]{1,0:T(8,128)(2,1)S(1)} %collective-permute-done.14.refs_1_), channel_id=1, source_target_pairs={{2,4},{4,2},{6,0},{0,6},{3,5},{5,3},{7,1},{1,7},{10,12},{12,10},{1... | collective-permute-start | bytes 393224 | tf_op jit(solution)/shard_map/ppermute | solution.py:346
  84.9 0.0 collective-permute-done.20.refs_5_.refs_9_
  84.9 0.8 collective-permute-start.15
  85.7 0.4 shard_map.78.refs_10_
  86.1 0.0 collective-permute-done.19.refs_4_.refs_8_
  86.1 0.7 shard_map.79.refs_5_
  86.8 0.0 collective-permute-done.17.refs_4_
  86.8 2.8 %collective-permute-done.16.refs_3_ = bf16[512,128]{1,0:T(8,128)(2,1)S(1)} collective-permute-done((bf16[512,128]{1,0:T(8,128)(2,1)S(1)}, bf16[512,128]{1,0:T(8,128)(2,1)S(1)}, u32[]{:S(2)}, u32[]{:S(2)}) %collective-permute-start.16) | collective-permute-done | bytes 131104 | tf_op jit(solution)/shard_map/ppermute | solution.py:346
  89.7 0.2 collective-permute-done.15.refs_2_
  89.9 1.2 %shard_map.80 = bf16[512,512]{1,0:T(8,128)(2,1)} custom-call(bf16[1024,512]{1,0:T(8,128)(2,1)S(1)} %collective-permute-done.refs_1_.refs_0_, bf16[512,128]{1,0:T(8,128)(2,1)S(1)} %collective-permute-done.14.refs_1_, bf16[512,128]{1,0:T(8,128)(2,1)S(1)} %collective-permute-done.15.refs_2_, bf16[512,128]{1,0:T(8,128)(2,1)S(1)} %collective-permute-done.16.refs_3_, ...), custom_call_target="tpu_custom_call" | custom-call | flops 268435456 | bytes 3145728 | tf_op jit(solution)/shard_map/pallas_call | solution.py:56
  (17 shorter events, 0.0 us)
Async XLA Ops:
  0.0 14.0 %collective-permute-start.7 = (bf16[512,512]{1,0:T(8,128)(2,1)}, bf16[512,512]{1,0:T(8,128)(2,1)}, u32[]{:S(2)}, u32[]{:S(2)}) collective-permute-start(bf16[512,512]{1,0:T(8,128)(2,1)} %refs_0_.9), channel_id=1, source_target_pairs={{0,2},{2,0},{4,6},{6,4},{1,3},{3,1},{5,7},{7,5},{8,10},{10,8},{12,... | collective-permute-start | bytes 1572872 | tf_op jit(solution)/shard_map/ppermute | solution.py:308
  1.6 17.2 %collective-permute-start.2 = (bf16[512,512]{1,0:T(8,128)(2,1)}, bf16[512,512]{1,0:T(8,128)(2,1)S(1)}, u32[]{:S(2)}, u32[]{:S(2)}) collective-permute-start(bf16[512,512]{1,0:T(8,128)(2,1)} %refs_0_.9), channel_id=1, source_target_pairs={{0,1},{1,0},{2,3},{3,2},{4,5},{5,4},{6,7},{7,6},{8,9},{9,8},{10,11... | collective-permute-start | bytes 1572872 | tf_op jit(solution)/shard_map/ppermute | solution.py:309
  3.7 5.9 %copy-start.7 = (f32[512]{0:T(512)S(1)}, f32[512]{0:T(512)}, u32[]{:S(2)}) copy-start(f32[512]{0:T(512)} %param.7) | copy-start | bytes 6148
  7.3 16.1 %collective-permute-start.1 = (bf16[512,512]{1,0:T(8,128)(2,1)}, bf16[512,512]{1,0:T(8,128)(2,1)S(1)}, u32[]{:S(2)}, u32[]{:S(2)}) collective-permute-start(bf16[512,512]{1,0:T(8,128)(2,1)} %shard_map.64), channel_id=1, source_target_pairs={{2,4},{4,2},{6,0},{0,6},{3,5},{5,3},{7,1},{1,7},{10,12},{12,10},{1... | collective-permute-start | bytes 1572872 | tf_op jit(solution)/shard_map/ppermute | solution.py:311
  9.6 1.2 %copy-start = (bf16[512,1024]{1,0:T(8,128)(2,1)S(1)}, bf16[512,1024]{1,0:T(8,128)(2,1)}, u32[]{:S(2)}) copy-start(bf16[512,1024]{1,0:T(8,128)(2,1)} %k_ref.11) | copy-start | bytes 3145732
  10.8 1.2 %copy-start.2 = (bf16[512,1024]{1,0:T(8,128)(2,1)S(1)}, bf16[512,1024]{1,0:T(8,128)(2,1)}, u32[]{:S(2)}) copy-start(bf16[512,1024]{1,0:T(8,128)(2,1)} %v_ref.11) | copy-start | bytes 3145732
  12.1 6.8 %copy-start.4 = (bf16[512,1024]{1,0:T(8,128)(2,1)S(1)}, bf16[512,1024]{1,0:T(8,128)(2,1)}, u32[]{:S(2)}) copy-start(bf16[512,1024]{1,0:T(8,128)(2,1)} %q_ref.11) | copy-start | bytes 3145732
  12.4 14.9 %collective-permute-start.6 = (bf16[512,512]{1,0:T(8,128)(2,1)S(1)}, bf16[512,512]{1,0:T(8,128)(2,1)S(1)}, u32[]{:S(2)}, u32[]{:S(2)}) collective-permute-start(bf16[512,512]{1,0:T(8,128)(2,1)S(1)} %get-tuple-element.15), channel_id=1, source_target_pairs={{0,2},{2,0},{4,6},{6,4},{1,3},{3,1},{5,7},{7,5},{8,10},{10,8},{12,... | collective-permute-start | bytes 1572872 | tf_op jit(solution)/shard_map/ppermute | solution.py:322
  14.0 16.5 %collective-permute-start.8 = (bf16[512,512]{1,0:T(8,128)(2,1)}, bf16[512,512]{1,0:T(8,128)(2,1)S(1)}, u32[]{:S(2)}, u32[]{:S(2)}) collective-permute-start(bf16[512,512]{1,0:T(8,128)(2,1)} %collective-permute-done.7.refs_1_), channel_id=1, source_target_pairs={{0,1},{1,0},{2,3},{3,2},{4,5},{5,4},{6,7},{7,6},{8,9},{9,8},{10,11... | collective-permute-start | bytes 1572872 | tf_op jit(solution)/shard_map/ppermute | solution.py:324
  16.6 6.8 %copy-start.6 = (bf16[1024,512]{1,0:T(8,128)(2,1)S(1)}, bf16[1024,512]{1,0:T(8,128)(2,1)}, u32[]{:S(2)}) copy-start(bf16[1024,512]{1,0:T(8,128)(2,1)} %refs_0_.11) | copy-start | bytes 3145732
  16.6 8.2 %copy-start.5 = (bf16[512,512]{1,0:T(8,128)(2,1)S(1)}, bf16[512,512]{1,0:T(8,128)(2,1)}, u32[]{:S(2)}) copy-start(bf16[512,512]{1,0:T(8,128)(2,1)} %refs_0_.9) | copy-start | bytes 1572868
  16.6 22.0 %collective-permute-start.12 = (bf16[512,512]{1,0:T(8,128)(2,1)S(1)}, bf16[512,512]{1,0:T(8,128)(2,1)S(1)}, u32[]{:S(2)}, u32[]{:S(2)}) collective-permute-start(bf16[512,512]{1,0:T(8,128)(2,1)S(1)} %get-tuple-element.20), channel_id=1, source_target_pairs={{0,2},{2,0},{4,6},{6,4},{1,3},{3,1},{5,7},{7,5},{8,10},{10,8},{12,... | collective-permute-start | bytes 1572872 | tf_op jit(solution)/shard_map/ppermute | solution.py:323
  19.3 11.2 %copy-start.1 = (bf16[512,1024]{1,0:T(8,128)(2,1)S(1)}, bf16[512,1024]{1,0:T(8,128)(2,1)}, u32[]{:S(2)}) copy-start(bf16[512,1024]{1,0:T(8,128)(2,1)} %k_ref.11) | copy-start | bytes 3145732
  19.3 11.2 %copy-start.3 = (bf16[512,1024]{1,0:T(8,128)(2,1)S(1)}, bf16[512,1024]{1,0:T(8,128)(2,1)}, u32[]{:S(2)}) copy-start(bf16[512,1024]{1,0:T(8,128)(2,1)} %v_ref.11) | copy-start | bytes 3145732
  19.3 21.2 %collective-permute-start.3 = (bf16[512,512]{1,0:T(8,128)(2,1)S(1)}, bf16[512,512]{1,0:T(8,128)(2,1)S(1)}, u32[]{:S(2)}, u32[]{:S(2)}) collective-permute-start(bf16[512,512]{1,0:T(8,128)(2,1)S(1)} %shard_map.66), channel_id=1, source_target_pairs={{2,4},{4,2},{6,0},{0,6},{3,5},{5,3},{7,1},{1,7},{10,12},{12,10},{1... | collective-permute-start | bytes 1572872 | tf_op jit(solution)/shard_map/ppermute | solution.py:313
  23.4 47.1 %collective-permute-start = (bf16[1024,512]{1,0:T(8,128)(2,1)S(1)}, bf16[1024,512]{1,0:T(8,128)(2,1)S(1)}, u32[]{:S(2)}, u32[]{:S(2)}) collective-permute-start(bf16[1024,512]{1,0:T(8,128)(2,1)S(1)} %copy-done.6), channel_id=1, source_target_pairs={{0,1},{1,0},{2,3},{3,2},{4,5},{5,4},{6,7},{7,6},{8,9},{9,8},{10,11... | collective-permute-start | bytes 3145736 | tf_op jit(solution)/shard_map/ppermute | solution.py:360
  27.3 14.9 %collective-permute-start.4 = (bf16[512,256]{1,0:T(8,128)(2,1)S(1)}, bf16[512,256]{1,0:T(8,128)(2,1)S(1)}, u32[]{:S(2)}, u32[]{:S(2)}) collective-permute-start(bf16[512,256]{1,0:T(8,128)(2,1)S(1)} %shard_map.68), channel_id=1, source_target_pairs={{0,2},{2,0},{4,6},{6,4},{1,3},{3,1},{5,7},{7,5},{8,10},{10,8},{12,... | collective-permute-start | bytes 786440 | tf_op jit(solution)/shard_map/ppermute | solution.py:314
  32.3 32.5 %collective-permute-start.9 = (bf16[1024,256]{1,0:T(8,128)(2,1)S(1)}, bf16[1024,256]{1,0:T(8,128)(2,1)S(1)}, u32[]{:S(2)}, u32[]{:S(2)}) collective-permute-start(bf16[1024,256]{1,0:T(8,128)(2,1)S(1)} %shard_map.71), channel_id=1, source_target_pairs={{2,4},{4,2},{6,0},{0,6},{3,5},{5,3},{7,1},{1,7},{10,12},{12,10},{1... | collective-permute-start | bytes 1572872 | tf_op jit(solution)/shard_map/ppermute | solution.py:337
  38.6 14.5 %collective-permute-start.10 = (bf16[528,256]{1,0:T(8,128)(2,1)S(1)}, bf16[528,256]{1,0:T(8,128)(2,1)S(1)}, u32[]{:S(2)}, u32[]{:S(2)}) collective-permute-start(bf16[528,256]{1,0:T(8,128)(2,1)S(1)} %get-tuple-element.18), channel_id=1, source_target_pairs={{2,4},{4,2},{6,0},{0,6},{3,5},{5,3},{7,1},{1,7},{10,12},{12,10},{1... | collective-permute-start | bytes 811016 | tf_op jit(solution)/shard_map/ppermute | solution.py:333
  40.5 15.5 %collective-permute-start.11 = (bf16[528,256]{1,0:T(8,128)(2,1)S(1)}, bf16[528,256]{1,0:T(8,128)(2,1)S(1)}, u32[]{:S(2)}, u32[]{:S(2)}) collective-permute-start(bf16[528,256]{1,0:T(8,128)(2,1)S(1)} %get-tuple-element.19), channel_id=1, source_target_pairs={{2,4},{4,2},{6,0},{0,6},{3,5},{5,3},{7,1},{1,7},{10,12},{12,10},{1... | collective-permute-start | bytes 811016 | tf_op jit(solution)/shard_map/ppermute | solution.py:335
  42.3 10.8 %collective-permute-start.5 = (bf16[512,256]{1,0:T(8,128)(2,1)S(1)}, bf16[512,256]{1,0:T(8,128)(2,1)S(1)}, u32[]{:S(2)}, u32[]{:S(2)}) collective-permute-start(bf16[512,256]{1,0:T(8,128)(2,1)S(1)} %shard_map.69), channel_id=1, source_target_pairs={{0,2},{2,0},{4,6},{6,4},{1,3},{3,1},{5,7},{7,5},{8,10},{10,8},{12,... | collective-permute-start | bytes 786440 | tf_op jit(solution)/shard_map/ppermute | solution.py:315
  58.2 6.6 %collective-permute-start.13 = (bf16[512,128]{1,0:T(8,128)(2,1)S(1)}, bf16[512,128]{1,0:T(8,128)(2,1)S(1)}, u32[]{:S(2)}, u32[]{:S(2)}) collective-permute-start(bf16[512,128]{1,0:T(8,128)(2,1)S(1)} %get-tuple-element.21), channel_id=1, source_target_pairs={{0,1},{1,0},{2,3},{3,2},{4,5},{5,4},{6,7},{7,6},{8,9},{9,8},{10,11... | collective-permute-start | bytes 393224 | tf_op jit(solution)/shard_map/ppermute | solution.py:352
  61.4 9.1 %collective-permute-start.23 = (bf16[512,128]{1,0:T(8,128)(2,1)S(1)}, bf16[512,128]{1,0:T(8,128)(2,1)S(1)}, u32[]{:S(2)}, u32[]{:S(2)}) collective-permute-start(bf16[512,128]{1,0:T(8,128)(2,1)S(1)} %get-tuple-element.24.refs_1_), channel_id=1, source_target_pairs={{0,4},{2,6},{4,0},{6,2},{1,5},{3,7},{5,1},{7,3},{8,12},{10,14},{12... | collective-permute-start | bytes 393224 | tf_op jit(solution)/shard_map/ppermute | solution.py:347
  63.7 10.3 %collective-permute-start.22 = (bf16[512,128]{1,0:T(8,128)(2,1)S(1)}, bf16[512,128]{1,0:T(8,128)(2,1)S(1)}, u32[]{:S(2)}, u32[]{:S(2)}) collective-permute-start(bf16[512,128]{1,0:T(8,128)(2,1)S(1)} %get-tuple-element.24.refs_1_), channel_id=1, source_target_pairs={{2,4},{4,2},{6,0},{0,6},{3,5},{5,3},{7,1},{1,7},{10,12},{12,10},{1... | collective-permute-start | bytes 393224 | tf_op jit(solution)/shard_map/ppermute | solution.py:346
  67.0 17.9 %collective-permute-start.20 = (bf16[512,256]{1,0:T(8,128)(2,1)S(1)}, bf16[512,256]{1,0:T(8,128)(2,1)S(1)}, u32[]{:S(2)}, u32[]{:S(2)}) collective-permute-start(bf16[512,256]{1,0:T(8,128)(2,1)S(1)} %get-tuple-element.23.refs_2_.refs_6_), channel_id=1, source_target_pairs={{0,4},{2,6},{4,0},{6,2},{1,5},{3,7},{5,1},{7,3},{8,12},{10,14},{12... | collective-permute-start | bytes 786440 | tf_op jit(solution)/shard_map/ppermute | solution.py:347
  69.9 16.2 %collective-permute-start.19 = (bf16[512,256]{1,0:T(8,128)(2,1)S(1)}, bf16[512,256]{1,0:T(8,128)(2,1)S(1)}, u32[]{:S(2)}, u32[]{:S(2)}) collective-permute-start(bf16[512,256]{1,0:T(8,128)(2,1)S(1)} %get-tuple-element.23.refs_2_.refs_6_), channel_id=1, source_target_pairs={{2,4},{4,2},{6,0},{0,6},{3,5},{5,3},{7,1},{1,7},{10,12},{12,10},{1... | collective-permute-start | bytes 786440 | tf_op jit(solution)/shard_map/ppermute | solution.py:346
  70.5 15.6 %collective-permute-start.18 = (bf16[512,256]{1,0:T(8,128)(2,1)S(1)}, bf16[512,256]{1,0:T(8,128)(2,1)S(1)}, u32[]{:S(2)}, u32[]{:S(2)}) collective-permute-start(bf16[512,256]{1,0:T(8,128)(2,1)S(1)} %get-tuple-element.23.refs_2_.refs_6_), channel_id=1, source_target_pairs={{0,2},{2,0},{4,6},{6,4},{1,3},{3,1},{5,7},{7,5},{8,10},{10,8},{12,... | collective-permute-start | bytes 786440 | tf_op jit(solution)/shard_map/ppermute | solution.py:345
  70.6 6.5 %collective-permute-start.14 = (bf16[512,128]{1,0:T(8,128)(2,1)S(1)}, bf16[512,128]{1,0:T(8,128)(2,1)S(1)}, u32[]{:S(2)}, u32[]{:S(2)}) collective-permute-start(bf16[512,128]{1,0:T(8,128)(2,1)S(1)} %get-tuple-element.22), channel_id=1, source_target_pairs={{0,1},{1,0},{2,3},{3,2},{4,5},{5,4},{6,7},{7,6},{8,9},{9,8},{10,11... | collective-permute-start | bytes 393224 | tf_op jit(solution)/shard_map/ppermute | solution.py:355
  73.9 9.5 %collective-permute-start.21 = (bf16[512,128]{1,0:T(8,128)(2,1)S(1)}, bf16[512,128]{1,0:T(8,128)(2,1)S(1)}, u32[]{:S(2)}, u32[]{:S(2)}) collective-permute-start(bf16[512,128]{1,0:T(8,128)(2,1)S(1)} %get-tuple-element.24.refs_1_), channel_id=1, source_target_pairs={{0,2},{2,0},{4,6},{6,4},{1,3},{3,1},{5,7},{7,5},{8,10},{10,8},{12,... | collective-permute-start | bytes 393224 | tf_op jit(solution)/shard_map/ppermute | solution.py:345
  77.1 9.8 %collective-permute-start.17 = (bf16[512,128]{1,0:T(8,128)(2,1)S(1)}, bf16[512,128]{1,0:T(8,128)(2,1)S(1)}, u32[]{:S(2)}, u32[]{:S(2)}) collective-permute-start(bf16[512,128]{1,0:T(8,128)(2,1)S(1)} %collective-permute-done.14.refs_1_), channel_id=1, source_target_pairs={{0,4},{2,6},{4,0},{6,2},{1,5},{3,7},{5,1},{7,3},{8,12},{10,14},{12... | collective-permute-start | bytes 393224 | tf_op jit(solution)/shard_map/ppermute | solution.py:347
  83.5 6.2 %collective-permute-start.16 = (bf16[512,128]{1,0:T(8,128)(2,1)S(1)}, bf16[512,128]{1,0:T(8,128)(2,1)S(1)}, u32[]{:S(2)}, u32[]{:S(2)}) collective-permute-start(bf16[512,128]{1,0:T(8,128)(2,1)S(1)} %collective-permute-done.14.refs_1_), channel_id=1, source_target_pairs={{2,4},{4,2},{6,0},{0,6},{3,5},{5,3},{7,1},{1,7},{10,12},{12,10},{1... | collective-permute-start | bytes 393224 | tf_op jit(solution)/shard_map/ppermute | solution.py:346
  84.9 5.0 %collective-permute-start.15 = (bf16[512,128]{1,0:T(8,128)(2,1)S(1)}, bf16[512,128]{1,0:T(8,128)(2,1)S(1)}, u32[]{:S(2)}, u32[]{:S(2)}) collective-permute-start(bf16[512,128]{1,0:T(8,128)(2,1)S(1)} %collective-permute-done.14.refs_1_), channel_id=1, source_target_pairs={{0,2},{2,0},{4,6},{6,4},{1,3},{3,1},{5,7},{7,5},{8,10},{10,8},{12,... | collective-permute-start | bytes 393224 | tf_op jit(solution)/shard_map/ppermute | solution.py:345

commit v3 on v2

--- a/solution.py
+++ b/solution.py
@@ -51,12 +51,12 @@
     return (near_ref[...].astype(F32) * gain_ref[...]).astype(BF16)
 
 
-def local_call(body, shapes, operands, flops, mebibytes=10, in_specs=None, scratch=(), exps=0):
+def local_call(body, shapes, operands, flops, mebibytes=10, in_specs=None, scratch=(), exps=0, out_spec=VMEM):
     outs = [jax.ShapeDtypeStruct(shape, dtype) for shape, dtype in shapes]
     results = pl.pallas_call(
         body,
         in_specs=in_specs or [VMEM] * len(operands),
-        out_specs=[VMEM] * len(outs),
+        out_specs=[out_spec] * len(outs),
         out_shape=outs,
         scratch_shapes=list(scratch),
         cost_estimate=pl.CostEstimate(
@@ -72,7 +72,7 @@
 def first_queries(near, gain, q_weight):
     tokens, width = near.shape
 
-    def body(gain_ref, near_ref, q_ref, out_ref, here, held, sems):
+    def body(gain_ref, near_ref, q_ref, out_ref, here, held, ready, sems):
         place = ring()
         copies = [pltpu.make_async_copy(near_ref, here, sems.at[0])]
         for slot, target in enumerate((ACROSS, SECOND)):
@@ -91,7 +91,11 @@
         for slot in range(2):
             copies[slot + 1].wait()
             cut = slice(slot * PAIR, (slot + 1) * PAIR)
-            out_ref[:, cut] = dot(block, held[:, cut]).astype(BF16)
+            ready[:, cut] = dot(block, held[:, cut]).astype(BF16)
+            copies.append(pltpu.make_async_copy(ready.at[:, cut], out_ref.at[:, cut], sems.at[slot + 3]))
+            copies[-1].start()
+        for copy in copies[3:]:
+            copy.wait()
 
     return local_call(
         body,
@@ -103,8 +107,10 @@
         [
             pltpu.VMEM((tokens, width), BF16),
             pltpu.VMEM((width, 2 * PAIR), BF16),
-            pltpu.SemaphoreType.DMA((3,)),
+            pltpu.VMEM((tokens, 2 * PAIR), BF16),
+            pltpu.SemaphoreType.DMA((5,)),
         ],
+        out_spec=HBM,
     )
 
 
@@ -122,10 +128,7 @@
                     out_ref[:, start : start + HEAD_DIM] = (block.astype(F32) * factor).astype(BF16)
 
     return local_call(
-        body,
-        [((width, 2 * PAIR), BF16), ((width, 2 * PAIR), BF16)],
-        (gain, k_weight, v_weight),
-        8 * width * PAIR,
+        body, [((width, 2 * PAIR), BF16), ((width, 2 * PAIR), BF16)], (gain, k_weight, v_weight), 8 * width * PAIR
     )
 
 
@@ -262,7 +265,7 @@
     )
 
 
-def output_product(terms, weights, extra, out_dtype):
+def output_product(terms, weights, extra, out_dtype, last=False):
     tokens = terms[0][0].shape[0]
     columns = sum(x.shape[1] for x in weights[0])
     bounds = [0]
@@ -284,14 +287,29 @@
                 parts[0] if len(parts) == 1 else jnp.concatenate(parts, axis=1),
             )
 
-        total = None if extra is None else refs[-2][...]
-        for index in range(0, len(terms), 2):
-            (left, top), (right, bottom) = operand(index), operand(index + 1)
-            term = dot(
-                jnp.concatenate([left, right], axis=1), jnp.concatenate([top, bottom], axis=0)
-            )
-            total = term if total is None else total + term
-        refs[-1][...] = total.astype(out_dtype)
+        out_ref = refs[bounds[-1] + len(terms) + (extra is not None)]
+        steps = 2 if last else 1
+        size = tokens // steps
+        copies = []
+        for step in range(steps):
+            rows = slice(step * size, (step + 1) * size)
+            total = None if extra is None else refs[bounds[-1] + len(terms)][rows, :]
+            for index in range(0, len(terms), 2):
+                (left, top), (right, bottom) = operand(index), operand(index + 1)
+                term = dot(
+                    jnp.concatenate([left[rows, :], right[rows, :]], axis=1),
+                    jnp.concatenate([top, bottom], axis=0),
+                )
+                total = term if total is None else total + term
+            if last:
+                ready, sems = refs[-2:]
+                ready[rows, :] = total.astype(out_dtype)
+                copies.append(pltpu.make_async_copy(ready.at[rows], out_ref.at[rows], sems.at[step]))
+                copies[-1].start()
+            else:
+                out_ref[...] = total.astype(out_dtype)
+        for copy in copies:
+            copy.wait()
 
     return local_call(
         body,
@@ -299,6 +317,8 @@
         operands,
         2 * tokens * columns * HEAD_DIM * len(terms),
         12,
+        scratch=[pltpu.VMEM((tokens, columns), out_dtype), pltpu.SemaphoreType.DMA((2,))] if last else [],
+        out_spec=HBM if last else VMEM,
     )
 
 
@@ -312,9 +332,7 @@
     both = (ACROSS, SECOND)
     q_other = lax.ppermute(queries(both, other, gain, q_weight, None, BF16), "row", P2)
     end_own = lax.ppermute(queries((FIRST,), own, gain, q_weight, (q_own, 0), BF16), "row", P1)
-    end_other = lax.ppermute(
-        queries((FIRST,), other, gain, q_weight, (q_other, 0), BF16), "row", P1
-    )
+    end_other = lax.ppermute(queries((FIRST,), other, gain, q_weight, (q_other, 0), BF16), "row", P1)
     kept_q_own = queries((ME,), own, gain, q_weight, (q_own, 1), F32)
     kept_q_other = queries((ME,), other, gain, q_weight, (q_other, 1), F32)
 
@@ -325,9 +343,7 @@
     pairs = [(own, own1), (other, other1)]
 
     def partial(head, target, place, pairs, arrived, out_dtype, sums=False):
-        return keys_values(
-            head, target, place, pairs, gain, k_weight, v_weight, arrived, out_dtype, sums
-        )
+        return keys_values(head, target, place, pairs, gain, k_weight, v_weight, arrived, out_dtype, sums)
 
     value, sums_own = partial(0, SECOND, 0, pairs[:1], passed, BF16, True)
     far0_own = lax.ppermute(value, "row", P2)
@@ -340,12 +356,7 @@
     kept1 = partial(1, ME, 1, pairs, stay, F32)
 
     def from_all(value):
-        return [
-            value,
-            lax.ppermute(value, "row", P1),
-            lax.ppermute(value, "row", P2),
-            lax.ppermute(value, "row", OPP),
-        ]
+        return [value, lax.ppermute(value, "row", P1), lax.ppermute(value, "row", P2), lax.ppermute(value, "row", OPP)]
 
     q_parts = ((kept_q_own, kept_q_other), (end_own, end_other))
     other0, own0 = attend(0, *q_parts, kept0, far0, near_sums, far0, None)
@@ -364,7 +375,7 @@
     terms += [(x, 1, 0, 1, source) for source, x in enumerate(middle_all)]
     total = output_product(terms, [here, there], total, F32)
     terms = [(x, 0, 0, 1, source) for source, x in enumerate(partner1_all)]
-    return output_product(terms, [there], total, BF16)
+    return output_product(terms, [there], total, BF16, True)
 
 
 def solution(mesh):

time: 92.7 us -> 92.6 us (level)
  no operation moved by 1% of the time
where the time goes in v3:
time: 92.6 us; the launch traced here: 91.2 us
  starting transfers between devices  42.2 us (46%)
  waiting for transfers between devices  26.5 us (29%)
  Pallas kernels  19.6 us (21%)
  local copies, waits for them, and re-layouts  2.48 us (3%)
    pallas_call x17, Pallas kernels, local_call(): pl.pallas_call(body, in_specs=in_specs or [VMEM] * len(operands), out_spe...  19.6 us
    ppermute x3, starting transfers between devices, from_all(): lax.ppermute(value, 'row', OPP)  9.2 us
    ppermute x1, waiting for transfers between devices, sublayer(): far0_own = lax.ppermute(value, 'row', P2)  7.08 us
    ppermute x3, waiting for transfers between devices, from_all(): lax.ppermute(value, 'row', P2)  4.28 us
    ppermute x1, starting transfers between devices, sublayer(): far1 = [lax.ppermute(partial(1, SECOND, 1, pairs, passed, BF16), 'row', P2)]  4.23 us
    ppermute x3, starting transfers between devices, from_all(): lax.ppermute(value, 'row', P2)  3.15 us
    ppermute x1, waiting for transfers between devices, sublayer(): far0_other = lax.ppermute(value, 'row', P2)  2.89 us
    ppermute x1, starting transfers between devices, sublayer(): other1 = lax.ppermute(own1, 'col', COL)  2.68 us
  transfers between devices with their start and end apart: 24, of which 11 were waited for; matrix products, arithmetic and copies ran while one was open for 0% of the time, Pallas kernels for 20%

profile of v3, /device:TPU:130, one launch (start us, length us, event | category | flops | bytes accessed | tf_op | source)
XLA Modules:
  0.0 91.2 jit_solution(5827781646693436077)
XLA Ops:
  0.0 1.6 %collective-permute-start.7 = (bf16[512,512]{1,0:T(8,128)(2,1)}, bf16[512,512]{1,0:T(8,128)(2,1)}, u32[]{:S(2)}, u32[]{:S(2)}) collective-permute-start(bf16[512,512]{1,0:T(8,128)(2,1)} %refs_0_.9), channel_id=1, source_target_pairs={{0,2},{2,0},{4,6},{6,4},{1,3},{3,1},{5,7},{7,5},{8,10},{10,8},{12,... | collective-permute-start | bytes 1572872 | tf_op jit(solution)/shard_map/ppermute | solution.py:328
  1.6 2.1 %collective-permute-start.2 = (bf16[512,512]{1,0:T(8,128)(2,1)}, bf16[512,512]{1,0:T(8,128)(2,1)S(1)}, u32[]{:S(2)}, u32[]{:S(2)}) collective-permute-start(bf16[512,512]{1,0:T(8,128)(2,1)} %refs_0_.9), channel_id=1, source_target_pairs={{0,1},{1,0},{2,3},{3,2},{4,5},{5,4},{6,7},{7,6},{8,9},{9,8},{10,11... | collective-permute-start | bytes 1572872 | tf_op jit(solution)/shard_map/ppermute | solution.py:329
  3.7 3.5 %shard_map.64 = bf16[512,512]{1,0:T(8,128)(2,1)} custom-call(f32[1,512]{1,0:T(1,128)} %bitcast.1, bf16[512,512]{1,0:T(8,128)(2,1)} %refs_0_.9, bf16[512,1024]{1,0:T(8,128)(2,1)} %q_ref.11), custom_call_target="tpu_custom_call" | custom-call | flops 268435456 | bytes 2099200 | tf_op jit(solution)/shard_map/pallas_call | solution.py:56
  7.3 2.3 %collective-permute-start.1 = (bf16[512,512]{1,0:T(8,128)(2,1)}, bf16[512,512]{1,0:T(8,128)(2,1)S(1)}, u32[]{:S(2)}, u32[]{:S(2)}) collective-permute-start(bf16[512,512]{1,0:T(8,128)(2,1)} %shard_map.64), channel_id=1, source_target_pairs={{2,4},{4,2},{6,0},{0,6},{3,5},{5,3},{7,1},{1,7},{10,12},{12,10},{1... | collective-permute-start | bytes 1572872 | tf_op jit(solution)/shard_map/ppermute | solution.py:331
  9.5 1.2 %copy-done = bf16[512,1024]{1,0:T(8,128)(2,1)S(1)} copy-done((bf16[512,1024]{1,0:T(8,128)(2,1)S(1)}, bf16[512,1024]{1,0:T(8,128)(2,1)}, u32[]{:S(2)}) %copy-start) | copy-done | bytes 1048600
  10.8 1.2 %copy-done.2 = bf16[512,1024]{1,0:T(8,128)(2,1)S(1)} copy-done((bf16[512,1024]{1,0:T(8,128)(2,1)S(1)}, bf16[512,1024]{1,0:T(8,128)(2,1)}, u32[]{:S(2)}) %copy-start.2) | copy-done | bytes 1048600
  12.0 0.4 shard_map.70
  12.4 0.8 collective-permute-start.6
  13.1 0.9 collective-permute-done.7.refs_1_
  14.0 2.7 %collective-permute-start.8 = (bf16[512,512]{1,0:T(8,128)(2,1)}, bf16[512,512]{1,0:T(8,128)(2,1)S(1)}, u32[]{:S(2)}, u32[]{:S(2)}) collective-permute-start(bf16[512,512]{1,0:T(8,128)(2,1)} %collective-permute-done.7.refs_1_), channel_id=1, source_target_pairs={{0,1},{1,0},{2,3},{3,2},{4,5},{5,4},{6,7},{7,6},{8,9},{9,8},{10,11... | collective-permute-start | bytes 1572872 | tf_op jit(solution)/shard_map/ppermute | solution.py:342
  16.7 2.2 %collective-permute-start.12 = (bf16[512,512]{1,0:T(8,128)(2,1)S(1)}, bf16[512,512]{1,0:T(8,128)(2,1)S(1)}, u32[]{:S(2)}, u32[]{:S(2)}) collective-permute-start(bf16[512,512]{1,0:T(8,128)(2,1)S(1)} %get-tuple-element.20), channel_id=1, source_target_pairs={{0,2},{2,0},{4,6},{6,4},{1,3},{3,1},{5,7},{7,5},{8,10},{10,8},{12,... | collective-permute-start | bytes 1572872 | tf_op jit(solution)/shard_map/ppermute | solution.py:341
  18.8 0.0 collective-permute-done.2.near_ref.refs_2_.refs_0_
  18.8 0.5 shard_map.66
  19.3 0.0 copy-start.1
  19.3 0.0 copy-start.3
  19.3 2.3 %collective-permute-start.3 = (bf16[512,512]{1,0:T(8,128)(2,1)S(1)}, bf16[512,512]{1,0:T(8,128)(2,1)S(1)}, u32[]{:S(2)}, u32[]{:S(2)}) collective-permute-start(bf16[512,512]{1,0:T(8,128)(2,1)S(1)} %shard_map.66), channel_id=1, source_target_pairs={{2,4},{4,2},{6,0},{0,6},{3,5},{5,3},{7,1},{1,7},{10,12},{12,10},{1... | collective-permute-start | bytes 1572872 | tf_op jit(solution)/shard_map/ppermute | solution.py:333
  21.6 1.7 %collective-permute-done.1.refs_0_ = bf16[512,512]{1,0:T(8,128)(2,1)S(1)} collective-permute-done((bf16[512,512]{1,0:T(8,128)(2,1)}, bf16[512,512]{1,0:T(8,128)(2,1)S(1)}, u32[]{:S(2)}, u32[]{:S(2)}) %collective-permute-start.1) | collective-permute-done | bytes 524320 | tf_op jit(solution)/shard_map/ppermute | solution.py:331
  23.2 1.4 %collective-permute-start = (bf16[1024,512]{1,0:T(8,128)(2,1)S(1)}, bf16[1024,512]{1,0:T(8,128)(2,1)S(1)}, u32[]{:S(2)}, u32[]{:S(2)}) collective-permute-start(bf16[1024,512]{1,0:T(8,128)(2,1)S(1)} %copy-done.6), channel_id=1, source_target_pairs={{0,1},{1,0},{2,3},{3,2},{4,5},{5,4},{6,7},{7,6},{8,9},{9,8},{10,11... | collective-permute-start | bytes 3145736 | tf_op jit(solution)/shard_map/ppermute | solution.py:371
  24.7 0.3 shard_map.68
  25.0 2.3 %collective-permute-done.6.arrived_ref = bf16[512,512]{1,0:T(8,128)(2,1)S(1)} collective-permute-done((bf16[512,512]{1,0:T(8,128)(2,1)S(1)}, bf16[512,512]{1,0:T(8,128)(2,1)S(1)}, u32[]{:S(2)}, u32[]{:S(2)}) %collective-permute-start.6) | collective-permute-done | bytes 524320 | tf_op jit(solution)/shard_map/ppermute | solution.py:340
  27.2 0.7 collective-permute-start.4
  27.9 2.6 %collective-permute-done.8.refs_3_.refs_1_ = bf16[512,512]{1,0:T(8,128)(2,1)S(1)} collective-permute-done((bf16[512,512]{1,0:T(8,128)(2,1)}, bf16[512,512]{1,0:T(8,128)(2,1)S(1)}, u32[]{:S(2)}, u32[]{:S(2)}) %collective-permute-start.8) | collective-permute-done | bytes 524320 | tf_op jit(solution)/shard_map/ppermute | solution.py:342
  30.5 1.8 %shard_map.71 = bf16[1024,256]{1,0:T(8,128)(2,1)S(1)} custom-call(f32[1,512]{1,0:T(1,128)S(1)} %bitcast.5, bf16[512,1024]{1,0:T(8,128)(2,1)S(1)} %copy-done.1, bf16[512,1024]{1,0:T(8,128)(2,1)S(1)} %copy-done.3, bf16[512,512]{1,0:T(8,128)(2,1)S(1)} %collective-permute-done.6.arrived_ref, bf16[512,512]{1,0:T(8,128)(2,1)S(1)} %copy-done.5, ...), custom_call_target="tpu_custom_call" | custom-call | flops 536870912 | bytes 5244928 | tf_op jit(solution)/shard_map/pallas_call | solution.py:56
  32.3 4.2 %collective-permute-start.9 = (bf16[1024,256]{1,0:T(8,128)(2,1)S(1)}, bf16[1024,256]{1,0:T(8,128)(2,1)S(1)}, u32[]{:S(2)}, u32[]{:S(2)}) collective-permute-start(bf16[1024,256]{1,0:T(8,128)(2,1)S(1)} %shard_map.71), channel_id=1, source_target_pairs={{2,4},{4,2},{6,0},{0,6},{3,5},{5,3},{7,1},{1,7},{10,12},{12,10},{1... | collective-permute-start | bytes 1572872 | tf_op jit(solution)/shard_map/ppermute | solution.py:353
  36.5 1.6 %shard_map.72 = (bf16[528,256]{1,0:T(8,128)(2,1)S(1)}, f32[1,512]{1,0:T(1,128)S(1)}) custom-call(f32[1,512]{1,0:T(1,128)S(1)} %bitcast.6, bf16[512,1024]{1,0:T(8,128)(2,1)S(1)} %copy-done.1, bf16[512,1024]{1,0:T(8,128)(2,1)S(1)} %copy-done.3, bf16[512,512]{1,0:T(8,128)(2,1)S(1)} %collective-permute-done.6.arrived_ref, bf16[512,512]{1,0:T(8,128)(2,1)S(1)} %copy-done.5, ...), custom_call_target="tpu_custom_call" | custom-call | flops 268435456 | bytes 3944448 | tf_op jit(solution)/shard_map/pallas_call | solution.py:56
  38.1 0.5 shard_map.73
  38.6 0.0 collective-permute-done.12.arrived_ref
  38.6 1.9 %collective-permute-start.10 = (bf16[528,256]{1,0:T(8,128)(2,1)S(1)}, bf16[528,256]{1,0:T(8,128)(2,1)S(1)}, u32[]{:S(2)}, u32[]{:S(2)}) collective-permute-start(bf16[528,256]{1,0:T(8,128)(2,1)S(1)} %get-tuple-element.18), channel_id=1, source_target_pairs={{2,4},{4,2},{6,0},{0,6},{3,5},{5,3},{7,1},{1,7},{10,12},{12,10},{1... | collective-permute-start | bytes 811016 | tf_op jit(solution)/shard_map/ppermute | solution.py:349
  40.5 0.0 collective-permute-done.3.refs_0_
  40.5 1.4 %collective-permute-start.11 = (bf16[528,256]{1,0:T(8,128)(2,1)S(1)}, bf16[528,256]{1,0:T(8,128)(2,1)S(1)}, u32[]{:S(2)}, u32[]{:S(2)}) collective-permute-start(bf16[528,256]{1,0:T(8,128)(2,1)S(1)} %get-tuple-element.19), channel_id=1, source_target_pairs={{2,4},{4,2},{6,0},{0,6},{3,5},{5,3},{7,1},{1,7},{10,12},{12,10},{1... | collective-permute-start | bytes 811016 | tf_op jit(solution)/shard_map/ppermute | solution.py:351
  41.9 0.3 shard_map.69
  42.3 1.3 %collective-permute-start.5 = (bf16[512,256]{1,0:T(8,128)(2,1)S(1)}, bf16[512,256]{1,0:T(8,128)(2,1)S(1)}, u32[]{:S(2)}, u32[]{:S(2)}) collective-permute-start(bf16[512,256]{1,0:T(8,128)(2,1)S(1)} %shard_map.69), channel_id=1, source_target_pairs={{0,2},{2,0},{4,6},{6,4},{1,3},{3,1},{5,7},{7,5},{8,10},{10,8},{12,... | collective-permute-start | bytes 786440 | tf_op jit(solution)/shard_map/ppermute | solution.py:335
  43.5 0.3 shard_map.65.refs_0_
  43.9 0.3 shard_map.67.refs_1_
  44.2 1.8 %shard_map.75.refs_10_ = f32[1024,256]{1,0:T(8,128)S(1)} custom-call(f32[1,512]{1,0:T(1,128)S(1)} %bitcast.11, bf16[512,1024]{1,0:T(8,128)(2,1)S(1)} %copy-done.1, bf16[512,1024]{1,0:T(8,128)(2,1)S(1)} %copy-done.3, bf16[512,512]{1,0:T(8,128)(2,1)S(1)} %collective-permute-done.12.arrived_ref, bf16[512,512]{1,0:T(8,128)(2,1)S(1)} %copy-done.5, ...), custom_call_target="tpu_custom_call" | custom-call | flops 536870912 | bytes 5769216 | tf_op jit(solution)/shard_map/pallas_call | solution.py:56
  45.9 7.1 %collective-permute-done.10.refs_4_.refs_8_.refs_7_ = bf16[528,256]{1,0:T(8,128)(2,1)S(1)} collective-permute-done((bf16[528,256]{1,0:T(8,128)(2,1)S(1)}, bf16[528,256]{1,0:T(8,128)(2,1)S(1)}, u32[]{:S(2)}, u32[]{:S(2)}) %collective-permute-start.10) | collective-permute-done | bytes 270368 | tf_op jit(solution)/shard_map/ppermute | solution.py:349
  53.0 2.9 %collective-permute-done.11.refs_5_.refs_9_.refs_8_ = bf16[528,256]{1,0:T(8,128)(2,1)S(1)} collective-permute-done((bf16[528,256]{1,0:T(8,128)(2,1)S(1)}, bf16[528,256]{1,0:T(8,128)(2,1)S(1)}, u32[]{:S(2)}, u32[]{:S(2)}) %collective-permute-start.11) | collective-permute-done | bytes 270368 | tf_op jit(solution)/shard_map/ppermute | solution.py:351
  55.9 2.2 %shard_map.76 = (bf16[512,128]{1,0:T(8,128)(2,1)S(1)}, bf16[512,128]{1,0:T(8,128)(2,1)S(1)}) custom-call(f32[512,256]{1,0:T(8,128)S(1)} %shard_map.65.refs_0_, f32[512,256]{1,0:T(8,128)S(1)} %shard_map.67.refs_1_, bf16[512,256]{1,0:T(8,128)(2,1)S(1)} %collective-permute-done.4.refs_2_, bf16[512,256]{1,0:T(8,128)(2,1)S(1)} %collective-permute-done.5.refs_3_, ...), custom_call_target="tpu_custom_call" | custom-call | flops 536870912 | bytes 3969024 | tf_op jit(solution)/shard_map/pallas_call | solution.py:56
  58.1 1.5 %collective-permute-start.13 = (bf16[512,128]{1,0:T(8,128)(2,1)S(1)}, bf16[512,128]{1,0:T(8,128)(2,1)S(1)}, u32[]{:S(2)}, u32[]{:S(2)}) collective-permute-start(bf16[512,128]{1,0:T(8,128)(2,1)S(1)} %get-tuple-element.21), channel_id=1, source_target_pairs={{0,1},{1,0},{2,3},{3,2},{4,5},{5,4},{6,7},{7,6},{8,9},{9,8},{10,11... | collective-permute-start | bytes 393224 | tf_op jit(solution)/shard_map/ppermute | solution.py:363
  59.6 1.7 %shard_map.74.refs_9_ = f32[1024,256]{1,0:T(8,128)S(1)} custom-call(f32[1,512]{1,0:T(1,128)S(1)} %bitcast.12, bf16[512,1024]{1,0:T(8,128)(2,1)S(1)} %copy-done.1, bf16[512,1024]{1,0:T(8,128)(2,1)S(1)} %copy-done.3, bf16[512,512]{1,0:T(8,128)(2,1)S(1)} %collective-permute-done.12.arrived_ref, bf16[512,512]{1,0:T(8,128)(2,1)S(1)} %copy-done.5, ...), custom_call_target="tpu_custom_call" | custom-call | flops 536870912 | bytes 5769216 | tf_op jit(solution)/shard_map/pallas_call | solution.py:56
  61.4 2.3 %collective-permute-start.23 = (bf16[512,128]{1,0:T(8,128)(2,1)S(1)}, bf16[512,128]{1,0:T(8,128)(2,1)S(1)}, u32[]{:S(2)}, u32[]{:S(2)}) collective-permute-start(bf16[512,128]{1,0:T(8,128)(2,1)S(1)} %get-tuple-element.24.refs_1_), channel_id=1, source_target_pairs={{0,4},{2,6},{4,0},{6,2},{1,5},{3,7},{5,1},{7,3},{8,12},{10,14},{12... | collective-permute-start | bytes 393224 | tf_op jit(solution)/shard_map/ppermute | solution.py:359
  63.7 1.1 %collective-permute-start.22 = (bf16[512,128]{1,0:T(8,128)(2,1)S(1)}, bf16[512,128]{1,0:T(8,128)(2,1)S(1)}, u32[]{:S(2)}, u32[]{:S(2)}) collective-permute-start(bf16[512,128]{1,0:T(8,128)(2,1)S(1)} %get-tuple-element.24.refs_1_), channel_id=1, source_target_pairs={{2,4},{4,2},{6,0},{0,6},{3,5},{5,3},{7,1},{1,7},{10,12},{12,10},{1... | collective-permute-start | bytes 393224 | tf_op jit(solution)/shard_map/ppermute | solution.py:359
  64.8 2.2 %shard_map.77 = (bf16[512,128]{1,0:T(8,128)(2,1)S(1)}, bf16[512,256]{1,0:T(8,128)(2,1)S(1)}) custom-call(f32[512,256]{1,0:T(8,128)S(1)} %shard_map.65.refs_0_, f32[512,256]{1,0:T(8,128)S(1)} %shard_map.67.refs_1_, bf16[512,256]{1,0:T(8,128)(2,1)S(1)} %collective-permute-done.4.refs_2_, bf16[512,256]{1,0:T(8,128)(2,1)S(1)} %collective-permute-done.5.refs_3_, ...), custom_call_target="tpu_custom_call" | custom-call | flops 536870912 | bytes 4214784 | tf_op jit(solution)/shard_map/pallas_call | solution.py:56
  67.0 2.9 %collective-permute-start.20 = (bf16[512,256]{1,0:T(8,128)(2,1)S(1)}, bf16[512,256]{1,0:T(8,128)(2,1)S(1)}, u32[]{:S(2)}, u32[]{:S(2)}) collective-permute-start(bf16[512,256]{1,0:T(8,128)(2,1)S(1)} %get-tuple-element.23.refs_2_.refs_6_), channel_id=1, source_target_pairs={{0,4},{2,6},{4,0},{6,2},{1,5},{3,7},{5,1},{7,3},{8,12},{10,14},{12... | collective-permute-start | bytes 786440 | tf_op jit(solution)/shard_map/ppermute | solution.py:359
  69.9 0.6 collective-permute-start.19
  70.5 0.0 collective-permute-done.refs_1_.refs_0_
  70.5 0.1 collective-permute-start.18
  70.6 0.0 collective-permute-done.23.refs_4_
  70.6 1.9 %collective-permute-start.14 = (bf16[512,128]{1,0:T(8,128)(2,1)S(1)}, bf16[512,128]{1,0:T(8,128)(2,1)S(1)}, u32[]{:S(2)}, u32[]{:S(2)}) collective-permute-start(bf16[512,128]{1,0:T(8,128)(2,1)S(1)} %get-tuple-element.22), channel_id=1, source_target_pairs={{0,1},{1,0},{2,3},{3,2},{4,5},{5,4},{6,7},{7,6},{8,9},{9,8},{10,11... | collective-permute-start | bytes 393224 | tf_op jit(solution)/shard_map/ppermute | solution.py:366
  72.5 1.5 %collective-permute-done.22.refs_3_ = bf16[512,128]{1,0:T(8,128)(2,1)S(1)} collective-permute-done((bf16[512,128]{1,0:T(8,128)(2,1)S(1)}, bf16[512,128]{1,0:T(8,128)(2,1)S(1)}, u32[]{:S(2)}, u32[]{:S(2)}) %collective-permute-start.22) | collective-permute-done | bytes 131104 | tf_op jit(solution)/shard_map/ppermute | solution.py:359
  73.9 0.9 collective-permute-start.21
  74.8 2.3 %collective-permute-done.14.refs_1_ = bf16[512,128]{1,0:T(8,128)(2,1)S(1)} collective-permute-done((bf16[512,128]{1,0:T(8,128)(2,1)S(1)}, bf16[512,128]{1,0:T(8,128)(2,1)S(1)}, u32[]{:S(2)}, u32[]{:S(2)}) %collective-permute-start.14) | collective-permute-done | bytes 131104 | tf_op jit(solution)/shard_map/ppermute | solution.py:366
  77.1 4.0 %collective-permute-start.17 = (bf16[512,128]{1,0:T(8,128)(2,1)S(1)}, bf16[512,128]{1,0:T(8,128)(2,1)S(1)}, u32[]{:S(2)}, u32[]{:S(2)}) collective-permute-start(bf16[512,128]{1,0:T(8,128)(2,1)S(1)} %collective-permute-done.14.refs_1_), channel_id=1, source_target_pairs={{0,4},{2,6},{4,0},{6,2},{1,5},{3,7},{5,1},{7,3},{8,12},{10,14},{12... | collective-permute-start | bytes 393224 | tf_op jit(solution)/shard_map/ppermute | solution.py:359
  81.1 2.4 %collective-permute-done.21.refs_2_ = bf16[512,128]{1,0:T(8,128)(2,1)S(1)} collective-permute-done((bf16[512,128]{1,0:T(8,128)(2,1)S(1)}, bf16[512,128]{1,0:T(8,128)(2,1)S(1)}, u32[]{:S(2)}, u32[]{:S(2)}) %collective-permute-start.21) | collective-permute-done | bytes 131104 | tf_op jit(solution)/shard_map/ppermute | solution.py:359
  83.5 1.4 %collective-permute-start.16 = (bf16[512,128]{1,0:T(8,128)(2,1)S(1)}, bf16[512,128]{1,0:T(8,128)(2,1)S(1)}, u32[]{:S(2)}, u32[]{:S(2)}) collective-permute-start(bf16[512,128]{1,0:T(8,128)(2,1)S(1)} %collective-permute-done.14.refs_1_), channel_id=1, source_target_pairs={{2,4},{4,2},{6,0},{0,6},{3,5},{5,3},{7,1},{1,7},{10,12},{12,10},{1... | collective-permute-start | bytes 393224 | tf_op jit(solution)/shard_map/ppermute | solution.py:359
  84.9 0.0 collective-permute-done.20.refs_5_.refs_9_
  84.9 0.8 collective-permute-start.15
  85.7 0.4 shard_map.78.refs_10_
  86.1 0.0 collective-permute-done.19.refs_4_.refs_8_
  86.1 0.7 shard_map.79.refs_5_
  86.8 0.0 collective-permute-done.17.refs_4_
  86.8 2.8 %collective-permute-done.16.refs_3_ = bf16[512,128]{1,0:T(8,128)(2,1)S(1)} collective-permute-done((bf16[512,128]{1,0:T(8,128)(2,1)S(1)}, bf16[512,128]{1,0:T(8,128)(2,1)S(1)}, u32[]{:S(2)}, u32[]{:S(2)}) %collective-permute-start.16) | collective-permute-done | bytes 131104 | tf_op jit(solution)/shard_map/ppermute | solution.py:359
  89.7 0.2 collective-permute-done.15.refs_2_
  89.9 1.2 %shard_map.80 = bf16[512,512]{1,0:T(8,128)(2,1)} custom-call(bf16[1024,512]{1,0:T(8,128)(2,1)S(1)} %collective-permute-done.refs_1_.refs_0_, bf16[512,128]{1,0:T(8,128)(2,1)S(1)} %collective-permute-done.14.refs_1_, bf16[512,128]{1,0:T(8,128)(2,1)S(1)} %collective-permute-done.15.refs_2_, bf16[512,128]{1,0:T(8,128)(2,1)S(1)} %collective-permute-done.16.refs_3_, ...), custom_call_target="tpu_custom_call" | custom-call | flops 268435456 | bytes 3145728 | tf_op jit(solution)/shard_map/pallas_call | solution.py:56
  (17 shorter events, 0.0 us)
Async XLA Ops:
  0.0 14.0 %collective-permute-start.7 = (bf16[512,512]{1,0:T(8,128)(2,1)}, bf16[512,512]{1,0:T(8,128)(2,1)}, u32[]{:S(2)}, u32[]{:S(2)}) collective-permute-start(bf16[512,512]{1,0:T(8,128)(2,1)} %refs_0_.9), channel_id=1, source_target_pairs={{0,2},{2,0},{4,6},{6,4},{1,3},{3,1},{5,7},{7,5},{8,10},{10,8},{12,... | collective-permute-start | bytes 1572872 | tf_op jit(solution)/shard_map/ppermute | solution.py:328
  1.6 17.2 %collective-permute-start.2 = (bf16[512,512]{1,0:T(8,128)(2,1)}, bf16[512,512]{1,0:T(8,128)(2,1)S(1)}, u32[]{:S(2)}, u32[]{:S(2)}) collective-permute-start(bf16[512,512]{1,0:T(8,128)(2,1)} %refs_0_.9), channel_id=1, source_target_pairs={{0,1},{1,0},{2,3},{3,2},{4,5},{5,4},{6,7},{7,6},{8,9},{9,8},{10,11... | collective-permute-start | bytes 1572872 | tf_op jit(solution)/shard_map/ppermute | solution.py:329
  3.7 5.8 %copy-start.7 = (f32[512]{0:T(512)S(1)}, f32[512]{0:T(512)}, u32[]{:S(2)}) copy-start(f32[512]{0:T(512)} %param.7) | copy-start | bytes 6148
  7.3 16.0 %collective-permute-start.1 = (bf16[512,512]{1,0:T(8,128)(2,1)}, bf16[512,512]{1,0:T(8,128)(2,1)S(1)}, u32[]{:S(2)}, u32[]{:S(2)}) collective-permute-start(bf16[512,512]{1,0:T(8,128)(2,1)} %shard_map.64), channel_id=1, source_target_pairs={{2,4},{4,2},{6,0},{0,6},{3,5},{5,3},{7,1},{1,7},{10,12},{12,10},{1... | collective-permute-start | bytes 1572872 | tf_op jit(solution)/shard_map/ppermute | solution.py:331
  9.5 1.2 %copy-start = (bf16[512,1024]{1,0:T(8,128)(2,1)S(1)}, bf16[512,1024]{1,0:T(8,128)(2,1)}, u32[]{:S(2)}) copy-start(bf16[512,1024]{1,0:T(8,128)(2,1)} %k_ref.11) | copy-start | bytes 3145732
  10.8 1.2 %copy-start.2 = (bf16[512,1024]{1,0:T(8,128)(2,1)S(1)}, bf16[512,1024]{1,0:T(8,128)(2,1)}, u32[]{:S(2)}) copy-start(bf16[512,1024]{1,0:T(8,128)(2,1)} %v_ref.11) | copy-start | bytes 3145732
  12.0 6.8 %copy-start.4 = (bf16[512,1024]{1,0:T(8,128)(2,1)S(1)}, bf16[512,1024]{1,0:T(8,128)(2,1)}, u32[]{:S(2)}) copy-start(bf16[512,1024]{1,0:T(8,128)(2,1)} %q_ref.11) | copy-start | bytes 3145732
  12.4 14.9 %collective-permute-start.6 = (bf16[512,512]{1,0:T(8,128)(2,1)S(1)}, bf16[512,512]{1,0:T(8,128)(2,1)S(1)}, u32[]{:S(2)}, u32[]{:S(2)}) collective-permute-start(bf16[512,512]{1,0:T(8,128)(2,1)S(1)} %get-tuple-element.15), channel_id=1, source_target_pairs={{0,2},{2,0},{4,6},{6,4},{1,3},{3,1},{5,7},{7,5},{8,10},{10,8},{12,... | collective-permute-start | bytes 1572872 | tf_op jit(solution)/shard_map/ppermute | solution.py:340
  14.0 16.5 %collective-permute-start.8 = (bf16[512,512]{1,0:T(8,128)(2,1)}, bf16[512,512]{1,0:T(8,128)(2,1)S(1)}, u32[]{:S(2)}, u32[]{:S(2)}) collective-permute-start(bf16[512,512]{1,0:T(8,128)(2,1)} %collective-permute-done.7.refs_1_), channel_id=1, source_target_pairs={{0,1},{1,0},{2,3},{3,2},{4,5},{5,4},{6,7},{7,6},{8,9},{9,8},{10,11... | collective-permute-start | bytes 1572872 | tf_op jit(solution)/shard_map/ppermute | solution.py:342
  16.7 6.6 %copy-start.6 = (bf16[1024,512]{1,0:T(8,128)(2,1)S(1)}, bf16[1024,512]{1,0:T(8,128)(2,1)}, u32[]{:S(2)}) copy-start(bf16[1024,512]{1,0:T(8,128)(2,1)} %refs_0_.11) | copy-start | bytes 3145732
  16.7 8.0 %copy-start.5 = (bf16[512,512]{1,0:T(8,128)(2,1)S(1)}, bf16[512,512]{1,0:T(8,128)(2,1)}, u32[]{:S(2)}) copy-start(bf16[512,512]{1,0:T(8,128)(2,1)} %refs_0_.9) | copy-start | bytes 1572868
  16.7 21.9 %collective-permute-start.12 = (bf16[512,512]{1,0:T(8,128)(2,1)S(1)}, bf16[512,512]{1,0:T(8,128)(2,1)S(1)}, u32[]{:S(2)}, u32[]{:S(2)}) collective-permute-start(bf16[512,512]{1,0:T(8,128)(2,1)S(1)} %get-tuple-element.20), channel_id=1, source_target_pairs={{0,2},{2,0},{4,6},{6,4},{1,3},{3,1},{5,7},{7,5},{8,10},{10,8},{12,... | collective-permute-start | bytes 1572872 | tf_op jit(solution)/shard_map/ppermute | solution.py:341
  19.3 11.2 %copy-start.1 = (bf16[512,1024]{1,0:T(8,128)(2,1)S(1)}, bf16[512,1024]{1,0:T(8,128)(2,1)}, u32[]{:S(2)}) copy-start(bf16[512,1024]{1,0:T(8,128)(2,1)} %k_ref.11) | copy-start | bytes 3145732
  19.3 11.2 %copy-start.3 = (bf16[512,1024]{1,0:T(8,128)(2,1)S(1)}, bf16[512,1024]{1,0:T(8,128)(2,1)}, u32[]{:S(2)}) copy-start(bf16[512,1024]{1,0:T(8,128)(2,1)} %v_ref.11) | copy-start | bytes 3145732
  19.3 21.2 %collective-permute-start.3 = (bf16[512,512]{1,0:T(8,128)(2,1)S(1)}, bf16[512,512]{1,0:T(8,128)(2,1)S(1)}, u32[]{:S(2)}, u32[]{:S(2)}) collective-permute-start(bf16[512,512]{1,0:T(8,128)(2,1)S(1)} %shard_map.66), channel_id=1, source_target_pairs={{2,4},{4,2},{6,0},{0,6},{3,5},{5,3},{7,1},{1,7},{10,12},{12,10},{1... | collective-permute-start | bytes 1572872 | tf_op jit(solution)/shard_map/ppermute | solution.py:333
  23.2 47.3 %collective-permute-start = (bf16[1024,512]{1,0:T(8,128)(2,1)S(1)}, bf16[1024,512]{1,0:T(8,128)(2,1)S(1)}, u32[]{:S(2)}, u32[]{:S(2)}) collective-permute-start(bf16[1024,512]{1,0:T(8,128)(2,1)S(1)} %copy-done.6), channel_id=1, source_target_pairs={{0,1},{1,0},{2,3},{3,2},{4,5},{5,4},{6,7},{7,6},{8,9},{9,8},{10,11... | collective-permute-start | bytes 3145736 | tf_op jit(solution)/shard_map/ppermute | solution.py:371
  27.2 15.0 %collective-permute-start.4 = (bf16[512,256]{1,0:T(8,128)(2,1)S(1)}, bf16[512,256]{1,0:T(8,128)(2,1)S(1)}, u32[]{:S(2)}, u32[]{:S(2)}) collective-permute-start(bf16[512,256]{1,0:T(8,128)(2,1)S(1)} %shard_map.68), channel_id=1, source_target_pairs={{0,2},{2,0},{4,6},{6,4},{1,3},{3,1},{5,7},{7,5},{8,10},{10,8},{12,... | collective-permute-start | bytes 786440 | tf_op jit(solution)/shard_map/ppermute | solution.py:334
  32.3 32.5 %collective-permute-start.9 = (bf16[1024,256]{1,0:T(8,128)(2,1)S(1)}, bf16[1024,256]{1,0:T(8,128)(2,1)S(1)}, u32[]{:S(2)}, u32[]{:S(2)}) collective-permute-start(bf16[1024,256]{1,0:T(8,128)(2,1)S(1)} %shard_map.71), channel_id=1, source_target_pairs={{2,4},{4,2},{6,0},{0,6},{3,5},{5,3},{7,1},{1,7},{10,12},{12,10},{1... | collective-permute-start | bytes 1572872 | tf_op jit(solution)/shard_map/ppermute | solution.py:353
  38.6 14.4 %collective-permute-start.10 = (bf16[528,256]{1,0:T(8,128)(2,1)S(1)}, bf16[528,256]{1,0:T(8,128)(2,1)S(1)}, u32[]{:S(2)}, u32[]{:S(2)}) collective-permute-start(bf16[528,256]{1,0:T(8,128)(2,1)S(1)} %get-tuple-element.18), channel_id=1, source_target_pairs={{2,4},{4,2},{6,0},{0,6},{3,5},{5,3},{7,1},{1,7},{10,12},{12,10},{1... | collective-permute-start | bytes 811016 | tf_op jit(solution)/shard_map/ppermute | solution.py:349
  40.5 15.4 %collective-permute-start.11 = (bf16[528,256]{1,0:T(8,128)(2,1)S(1)}, bf16[528,256]{1,0:T(8,128)(2,1)S(1)}, u32[]{:S(2)}, u32[]{:S(2)}) collective-permute-start(bf16[528,256]{1,0:T(8,128)(2,1)S(1)} %get-tuple-element.19), channel_id=1, source_target_pairs={{2,4},{4,2},{6,0},{0,6},{3,5},{5,3},{7,1},{1,7},{10,12},{12,10},{1... | collective-permute-start | bytes 811016 | tf_op jit(solution)/shard_map/ppermute | solution.py:351
  42.3 10.8 %collective-permute-start.5 = (bf16[512,256]{1,0:T(8,128)(2,1)S(1)}, bf16[512,256]{1,0:T(8,128)(2,1)S(1)}, u32[]{:S(2)}, u32[]{:S(2)}) collective-permute-start(bf16[512,256]{1,0:T(8,128)(2,1)S(1)} %shard_map.69), channel_id=1, source_target_pairs={{0,2},{2,0},{4,6},{6,4},{1,3},{3,1},{5,7},{7,5},{8,10},{10,8},{12,... | collective-permute-start | bytes 786440 | tf_op jit(solution)/shard_map/ppermute | solution.py:335
  58.1 6.7 %collective-permute-start.13 = (bf16[512,128]{1,0:T(8,128)(2,1)S(1)}, bf16[512,128]{1,0:T(8,128)(2,1)S(1)}, u32[]{:S(2)}, u32[]{:S(2)}) collective-permute-start(bf16[512,128]{1,0:T(8,128)(2,1)S(1)} %get-tuple-element.21), channel_id=1, source_target_pairs={{0,1},{1,0},{2,3},{3,2},{4,5},{5,4},{6,7},{7,6},{8,9},{9,8},{10,11... | collective-permute-start | bytes 393224 | tf_op jit(solution)/shard_map/ppermute | solution.py:363
  61.4 9.2 %collective-permute-start.23 = (bf16[512,128]{1,0:T(8,128)(2,1)S(1)}, bf16[512,128]{1,0:T(8,128)(2,1)S(1)}, u32[]{:S(2)}, u32[]{:S(2)}) collective-permute-start(bf16[512,128]{1,0:T(8,128)(2,1)S(1)} %get-tuple-element.24.refs_1_), channel_id=1, source_target_pairs={{0,4},{2,6},{4,0},{6,2},{1,5},{3,7},{5,1},{7,3},{8,12},{10,14},{12... | collective-permute-start | bytes 393224 | tf_op jit(solution)/shard_map/ppermute | solution.py:359
  63.7 10.3 %collective-permute-start.22 = (bf16[512,128]{1,0:T(8,128)(2,1)S(1)}, bf16[512,128]{1,0:T(8,128)(2,1)S(1)}, u32[]{:S(2)}, u32[]{:S(2)}) collective-permute-start(bf16[512,128]{1,0:T(8,128)(2,1)S(1)} %get-tuple-element.24.refs_1_), channel_id=1, source_target_pairs={{2,4},{4,2},{6,0},{0,6},{3,5},{5,3},{7,1},{1,7},{10,12},{12,10},{1... | collective-permute-start | bytes 393224 | tf_op jit(solution)/shard_map/ppermute | solution.py:359
  67.0 17.9 %collective-permute-start.20 = (bf16[512,256]{1,0:T(8,128)(2,1)S(1)}, bf16[512,256]{1,0:T(8,128)(2,1)S(1)}, u32[]{:S(2)}, u32[]{:S(2)}) collective-permute-start(bf16[512,256]{1,0:T(8,128)(2,1)S(1)} %get-tuple-element.23.refs_2_.refs_6_), channel_id=1, source_target_pairs={{0,4},{2,6},{4,0},{6,2},{1,5},{3,7},{5,1},{7,3},{8,12},{10,14},{12... | collective-permute-start | bytes 786440 | tf_op jit(solution)/shard_map/ppermute | solution.py:359
  69.9 16.2 %collective-permute-start.19 = (bf16[512,256]{1,0:T(8,128)(2,1)S(1)}, bf16[512,256]{1,0:T(8,128)(2,1)S(1)}, u32[]{:S(2)}, u32[]{:S(2)}) collective-permute-start(bf16[512,256]{1,0:T(8,128)(2,1)S(1)} %get-tuple-element.23.refs_2_.refs_6_), channel_id=1, source_target_pairs={{2,4},{4,2},{6,0},{0,6},{3,5},{5,3},{7,1},{1,7},{10,12},{12,10},{1... | collective-permute-start | bytes 786440 | tf_op jit(solution)/shard_map/ppermute | solution.py:359
  70.5 15.6 %collective-permute-start.18 = (bf16[512,256]{1,0:T(8,128)(2,1)S(1)}, bf16[512,256]{1,0:T(8,128)(2,1)S(1)}, u32[]{:S(2)}, u32[]{:S(2)}) collective-permute-start(bf16[512,256]{1,0:T(8,128)(2,1)S(1)} %get-tuple-element.23.refs_2_.refs_6_), channel_id=1, source_target_pairs={{0,2},{2,0},{4,6},{6,4},{1,3},{3,1},{5,7},{7,5},{8,10},{10,8},{12,... | collective-permute-start | bytes 786440 | tf_op jit(solution)/shard_map/ppermute | solution.py:359
  70.6 6.5 %collective-permute-start.14 = (bf16[512,128]{1,0:T(8,128)(2,1)S(1)}, bf16[512,128]{1,0:T(8,128)(2,1)S(1)}, u32[]{:S(2)}, u32[]{:S(2)}) collective-permute-start(bf16[512,128]{1,0:T(8,128)(2,1)S(1)} %get-tuple-element.22), channel_id=1, source_target_pairs={{0,1},{1,0},{2,3},{3,2},{4,5},{5,4},{6,7},{7,6},{8,9},{9,8},{10,11... | collective-permute-start | bytes 393224 | tf_op jit(solution)/shard_map/ppermute | solution.py:366
  73.9 9.5 %collective-permute-start.21 = (bf16[512,128]{1,0:T(8,128)(2,1)S(1)}, bf16[512,128]{1,0:T(8,128)(2,1)S(1)}, u32[]{:S(2)}, u32[]{:S(2)}) collective-permute-start(bf16[512,128]{1,0:T(8,128)(2,1)S(1)} %get-tuple-element.24.refs_1_), channel_id=1, source_target_pairs={{0,2},{2,0},{4,6},{6,4},{1,3},{3,1},{5,7},{7,5},{8,10},{10,8},{12,... | collective-permute-start | bytes 393224 | tf_op jit(solution)/shard_map/ppermute | solution.py:359
  77.1 9.8 %collective-permute-start.17 = (bf16[512,128]{1,0:T(8,128)(2,1)S(1)}, bf16[512,128]{1,0:T(8,128)(2,1)S(1)}, u32[]{:S(2)}, u32[]{:S(2)}) collective-permute-start(bf16[512,128]{1,0:T(8,128)(2,1)S(1)} %collective-permute-done.14.refs_1_), channel_id=1, source_target_pairs={{0,4},{2,6},{4,0},{6,2},{1,5},{3,7},{5,1},{7,3},{8,12},{10,14},{12... | collective-permute-start | bytes 393224 | tf_op jit(solution)/shard_map/ppermute | solution.py:359
  83.5 6.2 %collective-permute-start.16 = (bf16[512,128]{1,0:T(8,128)(2,1)S(1)}, bf16[512,128]{1,0:T(8,128)(2,1)S(1)}, u32[]{:S(2)}, u32[]{:S(2)}) collective-permute-start(bf16[512,128]{1,0:T(8,128)(2,1)S(1)} %collective-permute-done.14.refs_1_), channel_id=1, source_target_pairs={{2,4},{4,2},{6,0},{0,6},{3,5},{5,3},{7,1},{1,7},{10,12},{12,10},{1... | collective-permute-start | bytes 393224 | tf_op jit(solution)/shard_map/ppermute | solution.py:359
  84.9 5.0 %collective-permute-start.15 = (bf16[512,128]{1,0:T(8,128)(2,1)S(1)}, bf16[512,128]{1,0:T(8,128)(2,1)S(1)}, u32[]{:S(2)}, u32[]{:S(2)}) collective-permute-start(bf16[512,128]{1,0:T(8,128)(2,1)S(1)} %collective-permute-done.14.refs_1_), channel_id=1, source_target_pairs={{0,2},{2,0},{4,6},{6,4},{1,3},{3,1},{5,7},{7,5},{8,10},{10,8},{12,... | collective-permute-start | bytes 393224 | tf_op jit(solution)/shard_map/ppermute | solution.py:359
